TPU v7x, 32 devices: a whole 2x2x4 slice. The times are simulated.
32 devices in a mesh: shard: 8 (over z, x), grp: 4 (over y, core).
Axes of the slice: x: 2, y: 2, z: 4, core: 2. Of those that a mesh axis runs over, the one named last changes fastest.
Arguments:
- table_t: bfloat16 [100, 622592], P(None, ('shard', 'grp')), may hold values from -6 to 6
- req_rows: int32 [1024, 128], P(('shard', 'grp')), may hold values from 0 to 19455
- count1: int32 [1024], P(('shard', 'grp')), may hold values from 1 to 128, as said below
- frontier_list: int32 [11, 32768], P(None, ('shard', 'grp')), may hold values from 0 to 4095, as said below
- req2_rows: int32 [1024, 128], P(('shard', 'grp')), may hold values from 0 to 1023
- count2: int32 [1024], P(('shard', 'grp')), may hold values from 1 to 128, as said below
- seed_list: int32 [16, 8192], P(None, ('shard', 'grp')), may hold values from 0 to 4095, as said below
- w1_self: bfloat16 [256, 100], replicated, may hold values from -0.625 to 0.625
- w1_neigh: bfloat16 [256, 100], replicated, may hold values from -1.25 to 1.25
- bias1: float32 [256], replicated, may hold values from -3 to 3
- w2_self: bfloat16 [47, 256], replicated, may hold values from -0.375 to 0.375
- w2_neigh: bfloat16 [47, 256], replicated, may hold values from -0.75 to 0.75
- bias2: float32 [47], replicated, may hold values from -3 to 3
Outputs:
- logits: float32 [47, 8192], P(None, ('shard', 'grp'))
Inputs may be any that keep to these rules, and one draw needn't show every extreme that they name: count1[r * 32 + o] counts the live slots of the block that device r asks of device o; in every draw some devices are asked for 128 rows by every device. `frontier_list`: every entry o * 128 + j names a live slot (j below count1 of that block) of the asking device. count2[r * 32 + o] counts the live slots of the block that device r asks of device o; in every draw some devices are asked for 128 rows by every device. `seed_list`: every entry o * 128 + j names a live slot (j below count2 of that block) of the asking device.
All inputs are finite; a program needn't handle non-finite values.
Results may differ from a plain program's by a relative error of at most 0.0029.
Values may be sent and summed in bfloat16 or wider, within the bound.
No kernel may reach another device: no remote copies, remote signals or barrier semaphores. Data moves between devices by JAX's collectives and lax.ppermute only.
A program may use at most 64 MiB of HBM per device.

v0:
```python
import jax
import jax.numpy as jnp
from jax import lax
from jax.sharding import PartitionSpec as P


def mask_rows(received, counts, capacity):
    is_live = (jnp.arange(capacity, dtype=jnp.int32)[None, :] < counts[:, None]).reshape(-1)
    flat = received.reshape(-1, received.shape[-1])
    return jnp.where(is_live[:, None], flat, jnp.zeros((), flat.dtype))


def right_product(rows, weight):
    return lax.dot_general(
        rows, weight, (((1,), (1,)), ((), ())), preferred_element_type=jnp.float32
    )


def body(
    table_t,
    req_rows,
    count1,
    frontier_list,
    req2_rows,
    count2,
    seed_list,
    w1_self,
    w1_neigh,
    bias1,
    w2_self,
    w2_neigh,
    bias2,
):
    feat_width = table_t.shape[0]
    capacity = req_rows.shape[1]
    table_rows = table_t.T
    picked_rows = jnp.take(
        table_rows,
        lax.all_to_all(req_rows, ("shard", "grp"), split_axis=0, concat_axis=0, tiled=True),
        axis=0,
    )
    received = lax.all_to_all(
        picked_rows, ("shard", "grp"), split_axis=0, concat_axis=0, tiled=True
    )
    flat = mask_rows(received, count1, capacity)
    fanout_two = frontier_list.shape[0] - 1
    front_nodes = frontier_list.shape[1]
    picked = jnp.take(flat, frontier_list.reshape(-1), axis=0).reshape(
        fanout_two + 1, front_nodes, feat_width
    )
    summed = (jnp.sum(picked[1:].astype(jnp.float32), axis=0) / fanout_two).astype(jnp.bfloat16)
    preact = right_product(picked[0], w1_self) + right_product(summed, w1_neigh) + bias1[None, :]
    hidden_rows = jax.nn.relu(preact).astype(jnp.bfloat16)
    cap_two = req2_rows.shape[1]
    payload = jnp.concatenate(
        [right_product(hidden_rows, w2_self), right_product(hidden_rows, w2_neigh)], axis=1
    )
    chosen = jnp.take(
        payload,
        lax.all_to_all(req2_rows, ("shard", "grp"), split_axis=0, concat_axis=0, tiled=True),
        axis=0,
    )
    got_back = lax.all_to_all(chosen, ("shard", "grp"), split_axis=0, concat_axis=0, tiled=True)
    flat_two = mask_rows(got_back, count2, cap_two)
    fanout_one = seed_list.shape[0] - 1
    seed_nodes = seed_list.shape[1]
    picked_two = jnp.take(flat_two, seed_list.reshape(-1), axis=0).reshape(
        fanout_one + 1, seed_nodes, flat_two.shape[1]
    )
    classes = w2_self.shape[0]
    near = jnp.sum(picked_two[1:, :, classes:], axis=0) / fanout_one
    logits = (picked_two[0, :, :classes] + near).T + bias2[:, None]
    return logits


def solution(mesh):
    in_specs = (
        P(None, ("shard", "grp")),
        P(("shard", "grp"), None),
        P(("shard", "grp")),
        P(None, ("shard", "grp")),
        P(("shard", "grp"), None),
        P(("shard", "grp")),
        P(None, ("shard", "grp")),
        P(),
        P(),
        P(),
        P(),
        P(),
        P(),
    )
    out_specs = P(None, ("shard", "grp"))
    return jax.shard_map(body, mesh=mesh, in_specs=in_specs, out_specs=out_specs, check_vma=False)
```

profile of v0, /device:TPU:0, one launch (start us, length us, event | category | flops | bytes accessed | tf_op | source)
XLA Modules:
  0.0 196.0 jit_solution(5065027454529831224)
XLA Ops:
  0.0 7.3 %all-to-all-start.1 = ((s32[32,1,128]{2,1,0:T(1,128)}), s32[32,1,128]{2,1,0:T(1,128)S(1)}, u32[]{:S(2)}, u32[]{:S(2)}) async-start(s32[32,1,128]{2,1,0:T(1,128)} %bitcast.69), calls=%async_computation.1 | async-start | bytes 32768 | tf_op jit(solution)/shard_map/all_to_all | solution.py:39
  7.3 6.7 %copy.17 = bf16[100,19456]{0,1:T(8,128)(2,1)} copy(bf16[100,19456]{1,0:T(8,128)(2,1)} %param.13) | data formatting | bytes 7782400 | tf_op args[0]
  14.4 5.5 %all-to-all-start = ((s32[32,1,128]{2,1,0:T(1,128)}), s32[32,1,128]{2,1,0:T(1,128)S(1)}, u32[]{:S(2)}, u32[]{:S(2)}) async-start(s32[32,1,128]{2,1,0:T(1,128)} %bitcast.1), calls=%async_computation | async-start | bytes 32768 | tf_op jit(solution)/shard_map/all_to_all | solution.py:60
  19.9 14.1 %gather_fusion = bf16[4096,100]{1,0:T(8,128)(2,1)S(1)} fusion(bf16[19456,100]{1,0:T(8,128)(2,1)} %bitcast.54, s32[4096]{0:T(1024)S(1)} %fusion.10), kind=kCustom, calls=%fused_computation | custom fusion | bytes 1654784 | tf_op jit(solution)/shard_map/jit(_take)/gather | solution.py:37
  34.1 0.7 copy.18
  34.8 1.0 broadcast_select_fusion.1
  35.8 5.8 %all-to-all-start.2 = ((bf16[32,128,100]{1,2,0:T(8,128)(2,1)}), bf16[32,128,100]{1,2,0:T(8,128)(2,1)S(1)}, u32[]{:S(2)}, u32[]{:S(2)}) async-start(bf16[32,128,100]{1,2,0:T(8,128)(2,1)} %broadcast_select_fusion.1), calls=%async_computation.2 | async-start | bytes 1703936 | tf_op jit(solution)/shard_map/all_to_all | solution.py:42
  41.9 21.8 %all-to-all-done.2 = bf16[32,128,100]{1,2,0:T(8,128)(2,1)S(1)} async-done(((bf16[32,128,100]{1,2,0:T(8,128)(2,1)}), bf16[32,128,100]{1,2,0:T(8,128)(2,1)S(1)}, u32[]{:S(2)}, u32[]{:S(2)}) %all-to-all-start.2) | async-done | bytes 819232 | tf_op jit(solution)/shard_map/all_to_all | solution.py:42
  63.6 0.7 copy.19
  64.3 2.1 %bitcast_select_fusion.1 = bf16[4096,100]{1,0:T(8,128)(2,1)S(1)} fusion(bf16[32,128,100]{2,1,0:T(8,128)(2,1)S(1)} %copy.19, pred[4096]{0:T(1024)(128)(4,1)S(1)} %fusion.14), kind=kLoop, calls=%fused_computation.11 | loop fusion | flops 409600 | bytes 1642496 | tf_op jit(solution)/shard_map/jit(_where)/select_n | solution.py:10
  66.5 40.1 %gather_fusion.1 = bf16[11264,100]{1,0:T(8,128)(2,1)} fusion(bf16[4096,100]{1,0:T(8,128)(2,1)S(1)} %bitcast_select_fusion.1, s32[11264]{0:T(1024)S(1)} %broadcast_clamp_fusion), kind=kCustom, calls=%fused_computation.1 | custom fusion | bytes 4550656 | tf_op jit(solution)/shard_map/jit(_take)/gather | solution.py:48
  106.6 7.6 %broadcast_select_fusion = bf16[11264,100]{1,0:T(8,128)(2,1)S(1)} fusion(bf16[11264,100]{1,0:T(8,128)(2,1)} %gather_fusion.1, pred[11264]{0:T(1024)(128)(4,1)S(1)} %compare_and_fusion), kind=kLoop, calls=%fused_computation.5 | loop fusion | flops 1126400 | bytes 4516864 | tf_op jit(solution)/shard_map/jit(_take)/select_n | solution.py:48
  114.5 0.6 convert_reduce_fusion
  116.6 10.8 %gather_fusion.2 = f32[4096,94]{1,0:T(8,128)S(1)} fusion(f32[1024,94]{1,0:T(8,128)S(1)} %copy.20, s32[4096]{0:T(1024)S(1)} %fusion.12), kind=kCustom, calls=%fused_computation.2 | custom fusion | bytes 3096576 | tf_op jit(solution)/shard_map/jit(_take)/gather | solution.py:58
  127.4 1.8 copy.21
  129.2 2.8 %broadcast_select_fusion.3 = f32[32,128,94]{1,2,0:T(8,128)} fusion(f32[32,128,94]{1,2,0:T(8,128)} %copy.21, pred[32,128]{1,0:T(8,128)(4,1)S(1)} %compare_and_fusion.2), kind=kLoop, calls=%fused_computation.14 | loop fusion | flops 385024 | bytes 3084288 | tf_op jit(solution)/shard_map/jit(_take)/select_n | solution.py:58
  131.9 3.6 %all-to-all-start.3 = ((f32[32,128,94]{1,2,0:T(8,128)}), f32[32,128,94]{1,2,0:T(8,128)S(1)}, u32[]{:S(2)}, u32[]{:S(2)}) async-start(f32[32,128,94]{1,2,0:T(8,128)} %broadcast_select_fusion.3), calls=%async_computation.3 | async-start | bytes 3145728 | tf_op jit(solution)/shard_map/all_to_all | solution.py:63
  135.7 37.3 %all-to-all-done.3 = f32[32,128,94]{1,2,0:T(8,128)S(1)} async-done(((f32[32,128,94]{1,2,0:T(8,128)}), f32[32,128,94]{1,2,0:T(8,128)S(1)}, u32[]{:S(2)}, u32[]{:S(2)}) %all-to-all-start.3) | async-done | bytes 1540128 | tf_op jit(solution)/shard_map/all_to_all | solution.py:63
  173.0 1.9 copy.22
  174.9 3.6 %bitcast_select_fusion = f32[4096,94]{1,0:T(8,128)S(1)} fusion(f32[32,128,94]{2,1,0:T(8,128)} %copy.22, pred[4096]{0:T(1024)(128)(4,1)S(1)} %fusion.13), kind=kLoop, calls=%fused_computation.6 | loop fusion | flops 385024 | bytes 3084288 | tf_op jit(solution)/shard_map/jit(_where)/select_n | solution.py:10
  178.5 14.2 %gather_fusion.3 = f32[4096,94]{1,0:T(8,128)} fusion(f32[4096,94]{1,0:T(8,128)S(1)} %bitcast_select_fusion, s32[4096]{0:T(1024)S(1)} %broadcast_clamp_fusion.1), kind=kCustom, calls=%fused_computation.3 | custom fusion | bytes 3096576 | tf_op jit(solution)/shard_map/jit(_take)/gather | solution.py:67
  192.7 2.0 %copy.23 = f32[16,256,94]{1,2,0:T(8,128)S(1)} copy(f32[16,256,94]{2,1,0:T(8,128)} %bitcast.57) | data formatting | bytes 3080192 | tf_op jit(solution)/shard_map/jit(_take)/gather | solution.py:67
  194.9 0.4 copy-done.7
  195.3 0.7 fusion.8
  (45 shorter events, 2.7 us)
Async XLA Ops:
  0.0 115.0 %copy-start = (bf16[256,100]{0,1:T(8,128)(2,1)S(1)}, bf16[256,100]{0,1:T(8,128)(2,1)}, u32[]{:S(2)}) copy-start(bf16[256,100]{0,1:T(8,128)(2,1)} %param.20) | copy-start | bytes 153604
  0.0 14.4 %all-to-all-start.1 = ((s32[32,1,128]{2,1,0:T(1,128)}), s32[32,1,128]{2,1,0:T(1,128)S(1)}, u32[]{:S(2)}, u32[]{:S(2)}) async-start(s32[32,1,128]{2,1,0:T(1,128)} %bitcast.69), calls=%async_computation.1 | async-start | bytes 32768 | tf_op jit(solution)/shard_map/all_to_all | solution.py:39
  7.3 6.7 %copy-start.1 = (s32[11,1024]{1,0:T(8,128)S(1)}, s32[11,1024]{1,0:T(8,128)}, u32[]{:S(2)}) copy-start(s32[11,1024]{1,0:T(8,128)} %param.16) | copy-start | bytes 135172
  14.4 21.3 %all-to-all-start = ((s32[32,1,128]{2,1,0:T(1,128)}), s32[32,1,128]{2,1,0:T(1,128)S(1)}, u32[]{:S(2)}, u32[]{:S(2)}) async-start(s32[32,1,128]{2,1,0:T(1,128)} %bitcast.1), calls=%async_computation | async-start | bytes 32768 | tf_op jit(solution)/shard_map/all_to_all | solution.py:60
  34.7 7.0 %copy-start.8 = (s32[32]{0:T(128)S(1)}, s32[32]{0:T(128)}, u32[]{:S(2)}) copy-start(s32[32]{0:T(128)} %param.15) | copy-start | bytes 388
  35.8 27.8 %all-to-all-start.2 = ((bf16[32,128,100]{1,2,0:T(8,128)(2,1)}), bf16[32,128,100]{1,2,0:T(8,128)(2,1)S(1)}, u32[]{:S(2)}, u32[]{:S(2)}) async-start(bf16[32,128,100]{1,2,0:T(8,128)(2,1)} %broadcast_select_fusion.1), calls=%async_computation.2 | async-start | bytes 1703936 | tf_op jit(solution)/shard_map/all_to_all | solution.py:42
  114.4 0.9 copy-start.3
  114.5 0.9 copy-start.6
  115.1 0.7 copy-start.4
  115.1 1.0 copy-start.5
  131.9 3.6 %copy-start.2 = (s32[16,256]{1,0:T(8,128)S(1)}, s32[16,256]{1,0:T(8,128)}, u32[]{:S(2)}) copy-start(s32[16,256]{1,0:T(8,128)} %param.19) | copy-start | bytes 49156
  131.9 3.7 %copy-start.9 = (s32[32]{0:T(128)S(1)}, s32[32]{0:T(128)}, u32[]{:S(2)}) copy-start(s32[32]{0:T(128)} %param.18) | copy-start | bytes 388
  131.9 41.1 %all-to-all-start.3 = ((f32[32,128,94]{1,2,0:T(8,128)}), f32[32,128,94]{1,2,0:T(8,128)S(1)}, u32[]{:S(2)}, u32[]{:S(2)}) async-start(f32[32,128,94]{1,2,0:T(8,128)} %broadcast_select_fusion.3), calls=%async_computation.3 | async-start | bytes 3145728 | tf_op jit(solution)/shard_map/all_to_all | solution.py:63
  194.6 0.7 copy-start.7
where the time goes:
time: 197 us; the launch traced here: 196 us
  local copies, waits for them, and re-layouts  94 us (48%)
  waiting for transfers between devices  59.4 us (30%)
  starting transfers between devices  22.3 us (11%)
  other arithmetic  18.9 us (10%)
    gather x1, local copies, waits for them, and re-layouts, body(): jnp.take(flat, frontier_list.reshape(-1), axis=0)  40.1 us
    all_to_all x1, waiting for transfers between devices, body(): lax.all_to_all(chosen, ('shard', 'grp'), split_axis=0, concat_axis=0, til...  37.3 us
    all_to_all x1, waiting for transfers between devices, body(): lax.all_to_all(picked_rows, ('shard', 'grp'), split_axis=0, concat_axis=0...  21.8 us
    gather x2, local copies, waits for them, and re-layouts, body(): jnp.take(flat_two, seed_list.reshape(-1), axis=0)  16.2 us
    gather x2, local copies, waits for them, and re-layouts, body(): jnp.take(table_rows, lax.all_to_all(req_rows, ('shard', 'grp'), split_axi...  14.8 us
    gather x2, local copies, waits for them, and re-layouts, body(): jnp.take(payload, lax.all_to_all(req2_rows, ('shard', 'grp'), split_axis=...  12.6 us
    select_n x2, other arithmetic, body(): jnp.take(flat, frontier_list.reshape(-1), axis=0)  7.65 us
    unnamed x23, local copies, waits for them, and re-layouts  7.35 us
  transfers between devices with their start and end apart: 4, of which 3 were waited for; matrix products, arithmetic and copies ran while one was open for 12% of the time, Pallas kernels for 0%

commit v1 on v0

--- a/solution.py
+++ b/solution.py
@@ -1,7 +1,245 @@
+import functools
+
 import jax
 import jax.numpy as jnp
 from jax import lax
+from jax.experimental import pallas as pl
+from jax.experimental.pallas import tpu as pltpu
 from jax.sharding import PartitionSpec as P
+
+AXES = ("shard", "grp")
+F32 = jnp.float32
+BF16 = jnp.bfloat16
+I32 = jnp.int32
+WHOLE_VMEM = pl.BlockSpec(memory_space=pltpu.VMEM)
+WHOLE_SMEM = pl.BlockSpec(memory_space=pltpu.SMEM)
+IN_HBM = pl.BlockSpec(memory_space=pltpu.HBM)
+
+
+def exchange(blocks):
+    return lax.all_to_all(blocks, AXES, split_axis=0, concat_axis=0, tiled=True)
+
+
+def params(mib):
+    return pltpu.CompilerParams(vmem_limit_bytes=mib << 20)
+
+
+def identity(n, dtype):
+    rows = lax.broadcasted_iota(I32, (n, n), 0)
+    lanes = lax.broadcasted_iota(I32, (n, n), 1)
+    return jnp.where(rows == lanes, 1.0, 0.0).astype(dtype)
+
+
+def fetch_kernel(word_ref, asked_ref, pairs_hbm, out_ref, pairs, buf, sem):
+    blocks, feats, cap = out_ref.shape
+    load = pltpu.make_async_copy(pairs_hbm, pairs, sem)
+    load.start()
+    load.wait()
+
+    def gather(r, _):
+        for j in range(cap):
+            buf[r * cap + j] = pairs[word_ref[r, j] >> 17]
+        return 0
+
+    lax.fori_loop(0, blocks, gather, 0)
+    eye = identity(feats, BF16)
+    place = lax.broadcasted_iota(I32, (2 * cap, cap), 0).astype(F32).astype(BF16)
+    twice = 2 * lax.broadcasted_iota(I32, (1, cap), 1)
+
+    def turn(i, _):
+        for u in range(4):
+            r = i * 4 + u
+            x = buf[pl.ds(pl.multiple_of(r * cap, cap), cap)].reshape(2 * cap, feats)
+            y = lax.dot_general(eye, x, (((1,), (1,)), ((), ())), preferred_element_type=F32).astype(BF16)
+            want = twice + ((asked_ref[pl.ds(r, 1), :] >> 16) & 1)
+            want = jnp.broadcast_to(want.astype(F32), (2 * cap, cap)).astype(BF16)
+            pick = jnp.where(want == place, jnp.ones((), BF16), jnp.zeros((), BF16))
+            out_ref[r] = jnp.dot(y, pick, preferred_element_type=F32).astype(BF16)
+        return 0
+
+    lax.fori_loop(0, blocks // 4, turn, 0)
+
+
+def fetch(asked, table_t):
+    feats, n = table_t.shape
+    blocks, cap = asked.shape
+    pairs = table_t.T.reshape(n // 2, 2, feats)
+    return pl.pallas_call(
+        fetch_kernel,
+        out_shape=jax.ShapeDtypeStruct((blocks, feats, cap), BF16),
+        in_specs=[WHOLE_SMEM, WHOLE_VMEM, IN_HBM],
+        out_specs=WHOLE_VMEM,
+        scratch_shapes=[
+            pltpu.VMEM((n // 2, 2, feats), BF16),
+            pltpu.VMEM((blocks * cap, 2, feats), BF16),
+            pltpu.SemaphoreType.DMA,
+        ],
+        compiler_params=params(20),
+        name="fetch",
+    )(asked, asked, pairs)
+
+
+def own_weight(fanout):
+    return 1 << fanout.bit_length()
+
+
+def codes_kernel(own, count_ref, list_ref, out_ref):
+    depth, nodes = list_ref.shape
+    cap = out_ref.shape[0]
+    o = pl.program_id(0)
+    width = min(nodes, 256)
+    zero = jnp.zeros((16, width), BF16)
+    hit = [jnp.full((16, width), own if k == 0 else 1, BF16) for k in range(2)]
+
+    def step(t, _):
+        at = pl.multiple_of(t * width, width)
+        local = list_ref[:, pl.ds(at, width)] - o * cap
+        live = (local >= 0) & (local < count_ref[o])
+        local = jnp.where(live, local, -1).astype(F32)
+        want = [jnp.broadcast_to(local[k : k + 1], (16, width)).astype(BF16) for k in range(depth)]
+        for g in range(cap // 16):
+            slot = (lax.broadcasted_iota(I32, (16, width), 0) + g * 16).astype(F32).astype(BF16)
+            total = jnp.where(want[0] == slot, hit[0], zero)
+            for k in range(1, depth):
+                total = total + jnp.where(want[k] == slot, hit[1], zero)
+            out_ref[pl.ds(g * 16, 16), pl.ds(at, width)] = total
+        return 0
+
+    lax.fori_loop(0, nodes // width, step, 0)
+
+
+def codes(counts, lists, cap, place):
+    depth, nodes = lists.shape
+    blocks = counts.shape[0]
+    return pl.pallas_call(
+        functools.partial(codes_kernel, own_weight(depth - 1)),
+        grid=(blocks,),
+        out_shape=place((blocks * cap, nodes), BF16),
+        in_specs=[WHOLE_SMEM, WHOLE_VMEM],
+        out_specs=pl.BlockSpec((cap, nodes), lambda o: (o, 0)),
+        compiler_params=params(8),
+        name="codes",
+    )(counts, lists)
+
+
+def choose_kernel(group, word_ref, out_ref):
+    cap = word_ref.shape[1]
+    nodes = out_ref.shape[0]
+    one, zero = jnp.ones((16, cap), BF16), jnp.zeros((16, cap), BF16)
+    per = out_ref.shape[1] // cap
+    for u in range(per):
+        asked = word_ref[pl.ds(pl.program_id(0) * per + u, 1), :] & 0xFFFF
+        for base in range(0, nodes, group):
+            local = asked - base
+            local = jnp.where((local >= 0) & (local < group), local, -1).astype(F32)
+            want = jnp.broadcast_to(local, (16, cap)).astype(BF16)
+            for g in range(0, group, 16):
+                node = (lax.broadcasted_iota(I32, (16, cap), 0) + g).astype(F32).astype(BF16)
+                out_ref[pl.ds(base + g, 16), u * cap : (u + 1) * cap] = jnp.where(want == node, one, zero)
+
+
+def choose(asked, nodes):
+    blocks, cap = asked.shape
+    per = 4
+    return pl.pallas_call(
+        functools.partial(choose_kernel, 256),
+        grid=(blocks // per,),
+        out_shape=pltpu.HBM((nodes, blocks * cap), BF16),
+        in_specs=[WHOLE_VMEM],
+        out_specs=pl.BlockSpec((nodes, per * cap), lambda r: (0, r)),
+        compiler_params=params(8),
+        name="choose",
+    )(asked)
+
+
+def wide(ref, first, last, lo, hi):
+    return jnp.concatenate([ref[o, lo:hi] for o in range(first, last)], axis=1)
+
+
+def split_codes(code, own):
+    return jnp.where(code >= own, jnp.ones((), BF16), jnp.zeros((), BF16))
+
+
+def layer_kernel(
+    fanout, parts, got_ref, codes_hbm, choose_hbm, ws_ref, wn_ref, b_ref, w2_ref, out_ref, codes_v, choose_v, sems
+):
+    blocks, feats, cap = got_ref.shape
+    own_w = own_weight(fanout)
+    each = blocks // parts
+    span = each * cap
+    nodes = codes_v.shape[1]
+    loads = [
+        pltpu.make_async_copy(codes_hbm.at[pl.ds(i * span, span)], codes_v.at[pl.ds(i * span, span)], sems.at[i])
+        for i in range(parts)
+    ]
+    cap2 = out_ref.shape[2]
+    span2 = each * cap2
+    loads2 = [
+        pltpu.make_async_copy(
+            choose_hbm.at[:, pl.ds(i * span2, span2)], choose_v.at[:, pl.ds(i * span2, span2)], sems.at[parts + i]
+        )
+        for i in range(parts)
+    ]
+    for c in loads + loads2:
+        c.start()
+    own = jnp.zeros((feats, nodes), F32)
+    both = jnp.zeros((feats, nodes), F32)
+    for i in range(parts):
+        loads[i].wait()
+        got = wide(got_ref, i * each, (i + 1) * each, 0, feats)
+        code = codes_v[i * span : (i + 1) * span]
+        both = both + jnp.dot(got, code, preferred_element_type=F32)
+        own = own + jnp.dot(got, split_codes(code, own_w), preferred_element_type=F32)
+    summed = ((both - own_w * own) / fanout).astype(BF16)
+    pre = jnp.dot(ws_ref[...], own.astype(BF16), preferred_element_type=F32)
+    pre = pre + jnp.dot(wn_ref[...], summed, preferred_element_type=F32) + b_ref[...]
+    hidden = jnp.maximum(pre, 0.0).astype(BF16)
+    terms = jnp.dot(w2_ref[...], hidden, preferred_element_type=F32).astype(BF16)
+    for i in range(parts):
+        loads2[i].wait()
+        part = jnp.dot(terms, choose_v[:, i * span2 : (i + 1) * span2], preferred_element_type=F32).astype(BF16)
+        for r in range(each):
+            out_ref[i * each + r] = part[:, r * cap2 : (r + 1) * cap2]
+
+
+def layer(got, code, chosen, w1_self, w1_neigh, bias1, w2, fanout, cap):
+    blocks = got.shape[0]
+    parts = 8
+    return pl.pallas_call(
+        functools.partial(layer_kernel, fanout, parts),
+        out_shape=jax.ShapeDtypeStruct((blocks, w2.shape[0], cap), BF16),
+        in_specs=[WHOLE_VMEM, IN_HBM, IN_HBM] + [WHOLE_VMEM] * 4,
+        out_specs=WHOLE_VMEM,
+        scratch_shapes=[
+            pltpu.VMEM(code.shape, BF16),
+            pltpu.VMEM(chosen.shape, BF16),
+            pltpu.SemaphoreType.DMA((2 * parts,)),
+        ],
+        compiler_params=params(40),
+        name="layer",
+    )(got, code, chosen, w1_self, w1_neigh, bias1[:, None], w2)
+
+
+def logits_kernel(fanout, got_ref, code_ref, b_ref, out_ref):
+    blocks, half = got_ref.shape[0], got_ref.shape[1] // 2
+    classes = out_ref.shape[0]
+    own_w = own_weight(fanout)
+    code = code_ref[...]
+    own = split_codes(code, own_w)
+    mine = jnp.dot(wide(got_ref, 0, blocks, 0, half), own, preferred_element_type=F32)
+    near = jnp.dot(wide(got_ref, 0, blocks, half, 2 * half), code - own_w * own, preferred_element_type=F32) / fanout
+    out_ref[...] = (mine + near)[:classes] + b_ref[...]
+
+
+def final(got, code, bias2, fanout):
+    return pl.pallas_call(
+        functools.partial(logits_kernel, fanout),
+        out_shape=jax.ShapeDtypeStruct((bias2.shape[0], code.shape[1]), F32),
+        in_specs=[WHOLE_VMEM] * 3,
+        out_specs=WHOLE_VMEM,
+        compiler_params=params(20),
+        name="logits",
+    )(got, code, bias2[:, None])
 
 
 def mask_rows(received, counts, capacity):
@@ -16,7 +254,7 @@
     )
 
 
-def body(
+def plain_body(
     table_t,
     req_rows,
     count1,
@@ -36,11 +274,11 @@
     table_rows = table_t.T
     picked_rows = jnp.take(
         table_rows,
-        lax.all_to_all(req_rows, ("shard", "grp"), split_axis=0, concat_axis=0, tiled=True),
+        lax.all_to_all(req_rows, AXES, split_axis=0, concat_axis=0, tiled=True),
         axis=0,
     )
     received = lax.all_to_all(
-        picked_rows, ("shard", "grp"), split_axis=0, concat_axis=0, tiled=True
+        picked_rows, AXES, split_axis=0, concat_axis=0, tiled=True
     )
     flat = mask_rows(received, count1, capacity)
     fanout_two = frontier_list.shape[0] - 1
@@ -57,10 +295,10 @@
     )
     chosen = jnp.take(
         payload,
-        lax.all_to_all(req2_rows, ("shard", "grp"), split_axis=0, concat_axis=0, tiled=True),
+        lax.all_to_all(req2_rows, AXES, split_axis=0, concat_axis=0, tiled=True),
         axis=0,
     )
-    got_back = lax.all_to_all(chosen, ("shard", "grp"), split_axis=0, concat_axis=0, tiled=True)
+    got_back = lax.all_to_all(chosen, AXES, split_axis=0, concat_axis=0, tiled=True)
     flat_two = mask_rows(got_back, count2, cap_two)
     fanout_one = seed_list.shape[0] - 1
     seed_nodes = seed_list.shape[1]
@@ -73,21 +311,58 @@
     return logits
 
 
+MOST = 8 << 20
+
+
+def body(
+    table_t,
+    req_rows,
+    count1,
+    frontier_list,
+    req2_rows,
+    count2,
+    seed_list,
+    w1_self,
+    w1_neigh,
+    bias1,
+    w2_self,
+    w2_neigh,
+    bias2,
+):
+    cap = req_rows.shape[1]
+    fits = req_rows.size * frontier_list.shape[1] <= MOST and req2_rows.shape[1] == cap
+    if not fits or table_t.shape[1] > 32768 or frontier_list.shape[1] > 65536:
+        return plain_body(
+            table_t,
+            req_rows,
+            count1,
+            frontier_list,
+            req2_rows,
+            count2,
+            seed_list,
+            w1_self,
+            w1_neigh,
+            bias1,
+            w2_self,
+            w2_neigh,
+            bias2,
+        )
+    asked = exchange(req_rows * 65536 + req2_rows)
+    got1 = exchange(fetch(asked, table_t))
+    code1 = codes(count1, frontier_list, cap, pltpu.HBM)
+    chosen = choose(asked, frontier_list.shape[1])
+    classes = w2_self.shape[0]
+    half = -(-classes // 16) * 16
+    pad = ((0, half - classes), (0, 0))
+    w2 = jnp.concatenate([jnp.pad(w2_self, pad), jnp.pad(w2_neigh, pad)], axis=0)
+    out2 = layer(got1, code1, chosen, w1_self, w1_neigh, bias1, w2, frontier_list.shape[0] - 1, cap)
+    got2 = exchange(out2)
+    code2 = codes(count2, seed_list, cap, jax.ShapeDtypeStruct)
+    return final(got2, code2, bias2, seed_list.shape[0] - 1)
+
+
 def solution(mesh):
-    in_specs = (
-        P(None, ("shard", "grp")),
-        P(("shard", "grp"), None),
-        P(("shard", "grp")),
-        P(None, ("shard", "grp")),
-        P(("shard", "grp"), None),
-        P(("shard", "grp")),
-        P(None, ("shard", "grp")),
-        P(),
-        P(),
-        P(),
-        P(),
-        P(),
-        P(),
-    )
-    out_specs = P(None, ("shard", "grp"))
-    return jax.shard_map(body, mesh=mesh, in_specs=in_specs, out_specs=out_specs, check_vma=False)
+    split, split1 = P(AXES, None), P(AXES)
+    cols = P(None, AXES)
+    in_specs = (cols, split, split1, cols, split, split1, cols, P(), P(), P(), P(), P(), P())
+    return jax.shard_map(body, mesh=mesh, in_specs=in_specs, out_specs=cols, check_vma=False)

time: 197 us -> 98.1 us (0.50)
  local copies, waits for them, and re-layouts: 94 us -> 13 us
  Pallas kernels: 0 us -> 48.6 us
  waiting for transfers between devices: 59.4 us -> 15.8 us
  other arithmetic: 18.9 us -> 1.35 us
  starting transfers between devices: 22.3 us -> 18.6 us
    gather x7 -> x0, local copies, waits for them, and re-layouts: 83.6 us -> none  [the longest x1 40.1 us: body(): jnp.take(flat, frontier_list.reshape(-1), axis=0)]
    pallas_call x0 -> x6, Pallas kernels: none -> 48.6 us  [the longest x2 23.3 us: codes(): pl.pallas_call(functools.partial(codes_kernel, own_weight(depth - 1)), gr...]
    all_to_all x4 -> x3, waiting for transfers between devices: 59.4 us -> 15.8 us  [exchange(): return lax.all_to_all(blocks, AXES, split_axis=0, concat_axis=0, tiled=True)]
    select_n x8 -> x0, other arithmetic: 17.3 us -> none  [the longest x2 7.65 us: body(): jnp.take(flat, frontier_list.reshape(-1), axis=0)]
    transpose x0 -> x1, local copies, waits for them, and re-layouts: none -> 6.68 us  [fetch(): pairs = table_t.T.reshape(n // 2, 2, feats)]
    all_to_all x4 -> x3, starting transfers between devices: 22.3 us -> 18.6 us  [exchange(): return lax.all_to_all(blocks, AXES, split_axis=0, concat_axis=0, tiled=True)]
    all_to_all x2 -> x0, local copies, waits for them, and re-layouts: 2.55 us -> none  [the longest x1 1.86 us: body(): lax.all_to_all(chosen, ('shard', 'grp'), split_axis=0, concat_axis=0, til...]
    unnamed x23 -> x26, local copies, waits for them, and re-layouts: 7.35 us -> 6.08 us
  transfers between devices with their start and end apart: 4 -> 3, of which waited for: 3 -> 2; matrix products, arithmetic and copies ran while one was open for 12% -> 7% of each run, Pallas kernels for 0% -> 29%
where the time goes in v1:
time: 98.1 us; the launch traced here: 97.5 us
  Pallas kernels  48.6 us (50%)
  starting transfers between devices  18.6 us (19%)
  waiting for transfers between devices  15.8 us (16%)
  local copies, waits for them, and re-layouts  13 us (13%)
  other arithmetic  1.35 us (1%)
    pallas_call x2, Pallas kernels, codes(): pl.pallas_call(functools.partial(codes_kernel, own_weight(depth - 1)), gr...  23.3 us
    all_to_all x3, starting transfers between devices, exchange(): return lax.all_to_all(blocks, AXES, split_axis=0, concat_axis=0, tiled=True)  18.6 us
    all_to_all x3, waiting for transfers between devices, exchange(): return lax.all_to_all(blocks, AXES, split_axis=0, concat_axis=0, tiled=True)  15.8 us
    pallas_call x1, Pallas kernels, fetch(): pl.pallas_call(fetch_kernel, out_shape=jax.ShapeDtypeStruct((blocks, feat...  10.7 us
    pallas_call x1, Pallas kernels, layer(): pl.pallas_call(functools.partial(layer_kernel, fanout, parts), out_shape=...  7.72 us
    transpose x1, local copies, waits for them, and re-layouts, fetch(): pairs = table_t.T.reshape(n // 2, 2, feats)  6.68 us
    unnamed x26, local copies, waits for them, and re-layouts  6.08 us
    pallas_call x1, Pallas kernels, choose(): pl.pallas_call(functools.partial(choose_kernel, 256), grid=(blocks // per...  5.39 us
  transfers between devices with their start and end apart: 3, of which 2 were waited for; matrix products, arithmetic and copies ran while one was open for 7% of the time, Pallas kernels for 29%

profile of v1, /device:TPU:0, one launch (start us, length us, event | category | flops | bytes accessed | tf_op | source)
XLA Modules:
  0.0 97.5 jit_solution(12375053476332925458)
XLA Ops:
  0.0 1.3 %multiply_add_fusion = s32[32,128]{1,0:T(8,128)} fusion(s32[32,128]{1,0:T(8,128)} %param.17, s32[32,128]{1,0:T(8,128)} %param.14), kind=kLoop, calls=%fused_computation.5 | loop fusion | flops 8192 | bytes 49152 | tf_op jit(solution)/shard_map/add | solution.py:350
  1.3 7.3 %all-to-all-start = ((s32[32,1,128]{2,1,0:T(1,128)}), s32[32,1,128]{2,1,0:T(1,128)S(1)}, u32[]{:S(2)}, u32[]{:S(2)}) async-start(s32[32,1,128]{2,1,0:T(1,128)} %bitcast), calls=%async_computation | async-start | bytes 32768 | tf_op jit(solution)/shard_map/all_to_all | solution.py:20
  8.7 0.0 copy-start.6
  8.7 0.0 copy-start.7
  8.7 0.0 copy-start.2
  8.7 6.7 %copy.23 = bf16[19456,100]{1,0:T(8,128)(2,1)} copy(bf16[19456,100]{0,1:T(8,128)(2,1)} %bitcast.10) | data formatting | bytes 7782400 | tf_op jit(solution)/shard_map/transpose | solution.py:66
  15.4 0.4 all-to-all-done
  15.8 2.4 %copy-done.1 = bf16[19456,100]{1,0:T(8,128)(2,1)S(1)} copy-done((bf16[19456,100]{1,0:T(8,128)(2,1)S(1)}, bf16[19456,100]{1,0:T(8,128)(2,1)}, u32[]{:S(2)}) %copy-start.1) | copy-done | bytes 3891224
  18.2 10.7 %fetch.1 = bf16[32,100,128]{2,1,0:T(8,128)(2,1)} custom-call(s32[32,128]{1,0:T(8,128)S(1)} %bitcast.7, s32[32,128]{1,0:T(8,128)S(1)} %bitcast.8, bf16[9728,2,100]{2,1,0:T(2,128)(2,1)S(1)} %bitcast.6), custom_call_target="tpu_custom_call" | custom-call | tf_op jit(solution)/shard_map/fetch/pallas_call | solution.py:67
  28.9 0.0 copy-start.8
  28.9 0.0 copy-start.9
  29.0 5.5 %all-to-all-start.1 = ((bf16[32,100,128]{2,1,0:T(8,128)(2,1)}), bf16[32,100,128]{2,1,0:T(8,128)(2,1)S(1)}, u32[]{:S(2)}, u32[]{:S(2)}) async-start(bf16[32,100,128]{2,1,0:T(8,128)(2,1)} %fetch.1), calls=%async_computation.1 | async-start | bytes 1703936 | tf_op jit(solution)/shard_map/all_to_all | solution.py:20
  34.4 0.1 copy.26.b_ref
  34.6 0.1 copy.24.ws_ref
  34.7 0.1 copy.25.wn_ref
  34.9 18.2 %codes.2.codes_hbm = bf16[4096,1024]{1,0:T(8,128)(2,1)} custom-call(s32[32]{0:T(128)S(1)} %copy-done.4, s32[11,1024]{1,0:T(8,128)S(1)} %copy-done.2), custom_call_target="tpu_custom_call" | custom-call | tf_op jit(solution)/shard_map/codes/pallas_call | solution.py:114
  53.1 5.4 %choose.1.choose_hbm = bf16[1024,4096]{1,0:T(8,128)(2,1)} custom-call(s32[32,128]{1,0:T(8,128)S(1)} %bitcast.9), custom_call_target="tpu_custom_call" | custom-call | tf_op jit(solution)/shard_map/choose/pallas_call | solution.py:144
  58.5 3.4 %copy-done = bf16[4096,1024]{1,0:T(8,128)(2,1)S(1)} copy-done((bf16[4096,1024]{1,0:T(8,128)(2,1)S(1)}, bf16[4096,1024]{1,0:T(8,128)(2,1)}, u32[]{:S(2)}) %copy-start) | copy-done | bytes 8388632
  61.9 7.7 %layer.1 = bf16[32,96,128]{2,1,0:T(8,128)(2,1)} custom-call(bf16[32,100,128]{2,1,0:T(8,128)(2,1)S(1)} %all-to-all-done.1.got_ref, bf16[4096,1024]{1,0:T(8,128)(2,1)S(1)} %copy-done, bf16[1024,4096]{1,0:T(8,128)(2,1)} %choose.1.choose_hbm, bf16[256,100]{1,0:T(8,128)(2,1)S(1)} %copy.24.ws_ref, bf16[256,100]{1,0:T(8,128)(2,1)S(1)} %copy.25.wn_ref, ...), custom_call_target="tpu_custom_call" | custom-call | tf_op jit(solution)/shard_map/layer/pallas_call | solution.py:208
  69.6 5.8 %all-to-all-start.2 = ((bf16[32,96,128]{2,1,0:T(8,128)(2,1)}), bf16[32,96,128]{2,1,0:T(8,128)(2,1)S(1)}, u32[]{:S(2)}, u32[]{:S(2)}) async-start(bf16[32,96,128]{2,1,0:T(8,128)(2,1)} %layer.1), calls=%async_computation.2 | async-start | bytes 1572864 | tf_op jit(solution)/shard_map/all_to_all | solution.py:20
  75.5 0.1 copy.27.b_ref
  75.6 5.1 %codes.3.code_ref = bf16[4096,256]{1,0:T(8,128)(2,1)S(1)} custom-call(s32[32]{0:T(128)S(1)} %copy-done.5, s32[16,256]{1,0:T(8,128)S(1)} %copy-done.3), custom_call_target="tpu_custom_call" | custom-call | tf_op jit(solution)/shard_map/codes/pallas_call | solution.py:114
  80.7 15.4 %all-to-all-done.2.got_ref = bf16[32,96,128]{2,1,0:T(8,128)(2,1)S(1)} async-done(((bf16[32,96,128]{2,1,0:T(8,128)(2,1)}), bf16[32,96,128]{2,1,0:T(8,128)(2,1)S(1)}, u32[]{:S(2)}, u32[]{:S(2)}) %all-to-all-start.2) | async-done | bytes 786464 | tf_op jit(solution)/shard_map/all_to_all | solution.py:20
  96.0 1.5 %logits.1 = f32[47,256]{1,0:T(8,128)} custom-call(bf16[32,96,128]{2,1,0:T(8,128)(2,1)S(1)} %all-to-all-done.2.got_ref, bf16[4096,256]{1,0:T(8,128)(2,1)S(1)} %codes.3.code_ref, f32[47,1]{1,0:T(8,128)S(1)} %copy.27.b_ref), custom_call_target="tpu_custom_call" | custom-call | tf_op jit(solution)/shard_map/logits/pallas_call | solution.py:235
  (19 shorter events, 0.0 us)
Async XLA Ops:
  1.3 14.4 %all-to-all-start = ((s32[32,1,128]{2,1,0:T(1,128)}), s32[32,1,128]{2,1,0:T(1,128)S(1)}, u32[]{:S(2)}, u32[]{:S(2)}) async-start(s32[32,1,128]{2,1,0:T(1,128)} %bitcast), calls=%async_computation | async-start | bytes 32768 | tf_op jit(solution)/shard_map/all_to_all | solution.py:20
  8.7 25.9 %copy-start.6 = (bf16[256,100]{0,1:T(8,128)(2,1)S(1)}, bf16[256,100]{0,1:T(8,128)(2,1)}, u32[]{:S(2)}) copy-start(bf16[256,100]{0,1:T(8,128)(2,1)} %param.20) | copy-start | bytes 153604
  8.7 26.0 %copy-start.7 = (bf16[256,100]{0,1:T(8,128)(2,1)S(1)}, bf16[256,100]{0,1:T(8,128)(2,1)}, u32[]{:S(2)}) copy-start(bf16[256,100]{0,1:T(8,128)(2,1)} %param.21) | copy-start | bytes 153604
  8.7 26.2 %copy-start.2 = (s32[11,1024]{1,0:T(8,128)S(1)}, s32[11,1024]{1,0:T(8,128)}, u32[]{:S(2)}) copy-start(s32[11,1024]{1,0:T(8,128)} %list_ref.2) | copy-start | bytes 135172
  15.4 19.0 %copy-start.10 = (f32[256]{0:T(256)S(1)}, f32[256]{0:T(256)}, u32[]{:S(2)}) copy-start(f32[256]{0:T(256)} %param.22) | copy-start | bytes 3076
  15.4 19.5 %copy-start.4 = (s32[32]{0:T(128)S(1)}, s32[32]{0:T(128)}, u32[]{:S(2)}) copy-start(s32[32]{0:T(128)} %count_ref.2) | copy-start | bytes 388
  15.8 2.4 %copy-start.1 = (bf16[19456,100]{1,0:T(8,128)(2,1)S(1)}, bf16[19456,100]{1,0:T(8,128)(2,1)}, u32[]{:S(2)}) copy-start(bf16[19456,100]{1,0:T(8,128)(2,1)} %copy.23) | copy-start | bytes 11673604
  28.9 24.1 %copy-start.8 = (bf16[47,256]{1,0:T(8,128)(2,1)S(1)}, bf16[47,256]{1,0:T(8,128)(2,1)}, u32[]{:S(2)}) copy-start(bf16[47,256]{1,0:T(8,128)(2,1)} %param.24) | copy-start | bytes 72196
  28.9 24.1 %copy-start.9 = (bf16[47,256]{1,0:T(8,128)(2,1)S(1)}, bf16[47,256]{1,0:T(8,128)(2,1)}, u32[]{:S(2)}) copy-start(bf16[47,256]{1,0:T(8,128)(2,1)} %param.23) | copy-start | bytes 72196
  29.0 29.5 %all-to-all-start.1 = ((bf16[32,100,128]{2,1,0:T(8,128)(2,1)}), bf16[32,100,128]{2,1,0:T(8,128)(2,1)S(1)}, u32[]{:S(2)}, u32[]{:S(2)}) async-start(bf16[32,100,128]{2,1,0:T(8,128)(2,1)} %fetch.1), calls=%async_computation.1 | async-start | bytes 1703936 | tf_op jit(solution)/shard_map/all_to_all | solution.py:20
  58.5 3.4 %copy-start = (bf16[4096,1024]{1,0:T(8,128)(2,1)S(1)}, bf16[4096,1024]{1,0:T(8,128)(2,1)}, u32[]{:S(2)}) copy-start(bf16[4096,1024]{1,0:T(8,128)(2,1)} %codes.2.codes_hbm) | copy-start | bytes 25165828
  61.9 13.6 %copy-start.11 = (f32[47]{0:T(128)S(1)}, f32[47]{0:T(128)}, u32[]{:S(2)}) copy-start(f32[47]{0:T(128)} %param.25) | copy-start | bytes 568
  61.9 13.7 %copy-start.3 = (s32[16,256]{1,0:T(8,128)S(1)}, s32[16,256]{1,0:T(8,128)}, u32[]{:S(2)}) copy-start(s32[16,256]{1,0:T(8,128)} %list_ref.3) | copy-start | bytes 49156
  61.9 13.7 %copy-start.5 = (s32[32]{0:T(128)S(1)}, s32[32]{0:T(128)}, u32[]{:S(2)}) copy-start(s32[32]{0:T(128)} %count_ref.3) | copy-start | bytes 388
  69.6 26.4 %all-to-all-start.2 = ((bf16[32,96,128]{2,1,0:T(8,128)(2,1)}), bf16[32,96,128]{2,1,0:T(8,128)(2,1)S(1)}, u32[]{:S(2)}, u32[]{:S(2)}) async-start(bf16[32,96,128]{2,1,0:T(8,128)(2,1)} %layer.1), calls=%async_computation.2 | async-start | bytes 1572864 | tf_op jit(solution)/shard_map/all_to_all | solution.py:20

commit v2 on v1

v2 whole, which is shorter than its diff:
```python
import functools

import jax
import jax.numpy as jnp
from jax import lax
from jax.experimental import pallas as pl
from jax.experimental.pallas import tpu as pltpu
from jax.sharding import PartitionSpec as P

AXES = ("shard", "grp")
F32 = jnp.float32
BF16 = jnp.bfloat16
I32 = jnp.int32
WHOLE_VMEM = pl.BlockSpec(memory_space=pltpu.VMEM)
WHOLE_SMEM = pl.BlockSpec(memory_space=pltpu.SMEM)
IN_HBM = pl.BlockSpec(memory_space=pltpu.HBM)


def exchange(blocks):
    return lax.all_to_all(blocks, AXES, split_axis=0, concat_axis=0, tiled=True)


def params(mib):
    return pltpu.CompilerParams(vmem_limit_bytes=mib << 20)


def identity(n, dtype):
    rows = lax.broadcasted_iota(I32, (n, n), 0)
    lanes = lax.broadcasted_iota(I32, (n, n), 1)
    return jnp.where(rows == lanes, 1.0, 0.0).astype(dtype)


def fetch_kernel(
    parts, ahead, group, idx_ref, asked_hbm, table_hbm, out_hbm, cols, rows, even, odd, slots, out_v, asked_v, sems, out_sems, slot_sems
):
    feats, n = cols.shape
    blocks, rows_out, cap = out_v.shape
    span = n // parts
    loads = [
        pltpu.make_async_copy(
            table_hbm.at[:, pl.ds(i * span, span)], cols.at[:, pl.ds(i * span, span)], sems.at[i]
        )
        for i in range(parts)
    ]
    for c in loads[:ahead]:
        c.start()

    def refill(slot, first):
        return pltpu.make_async_copy(idx_ref.at[pl.ds(first, group)], slots[slot], slot_sems.at[slot])

    refill(0, 0).start()
    refill(1, group).start()
    ask = pltpu.make_async_copy(asked_hbm, asked_v, sems.at[parts])
    ask.start()
    wide = max(w for w in range(1, 9) if (span // 128) % w == 0)
    for i in range(parts):
        if i + ahead < parts:
            loads[i + ahead].start()
        loads[i].wait()

        def tile(t, _):
            for u in range(wide):
                at = pl.multiple_of(i * span + (t * wide + u) * 128, 128)
                rows[pl.ds(at, 128), :feats] = cols[:, pl.ds(at, 128)].astype(F32).T
            return 0

        lax.fori_loop(0, span // 128 // wide, tile, 0, unroll=True)

    ask.wait()
    base = feats // 16 * 16
    row = lax.broadcasted_iota(I32, (16, cap), 0)

    def gather(slot, u, buf):
        for j in range(cap):
            buf[pl.ds(j, 1), :] = rows[pl.ds(slots[slot][u, j], 1), :]

    def turn(r, buf):
        y = buf[...].T
        asked = asked_v[pl.ds(r, 1), :]
        high, low = (asked // cap).astype(F32), (asked % cap).astype(F32)
        tail = jnp.where(row == feats - base, high, jnp.where(row == feats - base + 1, low, y[base : base + 16]))
        out_v[r, :base] = y[:base].astype(BF16)
        out_v[r, base:] = tail[: rows_out - base].astype(BF16)

    def leave(i):
        return pltpu.make_async_copy(out_v.at[pl.ds(i * group, group)], out_hbm.at[pl.ds(i * group, group)], out_sems.at[i])

    trips = blocks // (2 * group)

    def many(i, _):
        for slot in range(2):
            first = (2 * i + slot) * group
            refill(slot, first).wait()
            for u in range(group):
                buf = (even, odd)[u % 2]
                gather(slot, u, buf)
                turn(first + u, buf)

            @pl.when(i + 1 < trips)
            def _():
                refill(slot, first + 2 * group).start()

            leave(2 * i + slot).start()
        return 0

    lax.fori_loop(0, trips, many, 0)
    for i in range(2 * trips):
        leave(i).wait()


def fetch(idx, asked, table_t):
    feats, n = table_t.shape
    blocks, cap = idx.shape
    parts = 8 if n % 1024 == 0 else 1
    group = 4
    return pl.pallas_call(
        functools.partial(fetch_kernel, parts, parts, group),
        out_shape=pltpu.HBM((blocks, feats + 2, cap), BF16),
        in_specs=[WHOLE_VMEM, IN_HBM, IN_HBM],
        out_specs=IN_HBM,
        scratch_shapes=[
            pltpu.VMEM((feats, n), BF16),
            pltpu.VMEM((n, 128), F32),
            pltpu.VMEM((cap, 128), F32),
            pltpu.VMEM((cap, 128), F32),
            [pltpu.SMEM((group, cap), I32), pltpu.SMEM((group, cap), I32)],
            pltpu.VMEM((blocks, feats + 2, cap), BF16),
            pltpu.VMEM((blocks, cap), I32),
            pltpu.SemaphoreType.DMA((parts + 1,)),
            pltpu.SemaphoreType.DMA((blocks // group,)),
            pltpu.SemaphoreType.DMA((2,)),
        ],
        compiler_params=params(40),
        name="fetch",
    )(idx, pltpu.with_memory_space_constraint(asked, pltpu.HBM), pltpu.with_memory_space_constraint(table_t, pltpu.HBM))


def own_weight(fanout):
    return 1 << fanout.bit_length()


def codes_kernel(own, cap, count_ref, list_ref, out_ref):
    depth, width = list_ref.shape
    each = out_ref.shape[1] // cap
    zero = jnp.zeros((16, width), BF16)
    hit = [jnp.full((16, width), own if k == 0 else 1, BF16) for k in range(2)]

    def step(t, _):
        o = pl.program_id(1) * each + t
        local = list_ref[...] - o * cap
        live = (local >= 0) & (local < count_ref[o])
        local = jnp.where(live, local, -1).astype(F32)
        want = [jnp.broadcast_to(local[k : k + 1], (16, width)).astype(BF16) for k in range(depth)]
        for g in range(cap // 16):
            slot = (lax.broadcasted_iota(I32, (16, width), 0) + g * 16).astype(F32).astype(BF16)
            total = jnp.where(want[0] == slot, hit[0], zero)
            for k in range(1, depth):
                total = total + jnp.where(want[k] == slot, hit[1], zero)
            out_ref[0, pl.ds(pl.multiple_of(t * cap + g * 16, 16), 16), :] = total
        return 0

    lax.fori_loop(0, each, step, 0)


def codes(counts, lists, cap, place):
    depth, nodes = lists.shape
    blocks = counts.shape[0]
    width = 256
    each = 8
    return pl.pallas_call(
        functools.partial(codes_kernel, own_weight(depth - 1), cap),
        grid=(nodes // width, blocks // each),
        out_shape=place((nodes // width, blocks * cap, width), BF16),
        in_specs=[WHOLE_SMEM, pl.BlockSpec((depth, width), lambda q, o: (0, q))],
        out_specs=pl.BlockSpec((1, each * cap, width), lambda q, o: (q, o, 0)),
        compiler_params=params(8),
        name="codes",
    )(counts, lists)


def split_codes(code, own):
    return jnp.where(code >= own, jnp.ones((), BF16), jnp.zeros((), BF16))


def layer_kernel(
    fanout, got_ref, first_ref, codes_hbm, ws_ref, wn_ref, b_ref, w2_ref, out_v, codes_v, got_v, choose_v, terms_v, sems
):
    blocks, _, cap = got_ref.shape
    feats = got_v.shape[0]
    rest, slots, width = codes_v.shape
    parts = rest + 1
    pairs, nodes, _ = choose_v.shape
    own_w = own_weight(fanout)
    def load(q):
        return pltpu.make_async_copy(codes_hbm.at[q], codes_v.at[q], sems.at[q])

    for q in range(rest):
        load(q).start()
    one, zero = jnp.ones((16, cap), BF16), jnp.zeros((16, cap), BF16)

    def choose(p, _):
        for u in range(2):
            o = 2 * p + u
            got_v[:, pl.ds(pl.multiple_of(o * cap, cap), cap)] = got_ref[o, :feats]
            asked = got_ref[o, feats : feats + 2].astype(F32)
            asked = asked[0:1] * cap + asked[1:2]
            for base in range(0, nodes, 256):
                local = asked - base
                local = jnp.where((local >= 0) & (local < 256), local, -1.0)
                want = jnp.broadcast_to(local, (16, cap)).astype(BF16)
                for g in range(0, 256, 16):
                    node = (lax.broadcasted_iota(I32, (16, cap), 0) + g).astype(F32).astype(BF16)
                    choose_v[p, base + g : base + g + 16, u * cap : (u + 1) * cap] = jnp.where(want == node, one, zero)
        return 0

    lax.fori_loop(0, pairs, choose, 0)
    for q in range(parts):
        if q:
            load(q - 1).wait()
        code = codes_v[q - 1] if q else first_ref[0]
        both = jnp.dot(got_v[...], code, preferred_element_type=F32)
        own = jnp.dot(got_v[...], split_codes(code, own_w), preferred_element_type=F32)
        summed = ((both - own_w * own) / fanout).astype(BF16)
        pre = jnp.dot(ws_ref[...], own.astype(BF16), preferred_element_type=F32)
        pre = pre + jnp.dot(wn_ref[...], summed, preferred_element_type=F32) + b_ref[...]
        hidden = jnp.maximum(pre, 0.0).astype(BF16)
        terms = jnp.dot(w2_ref[...], hidden, preferred_element_type=F32)
        terms_v[:, q * width : (q + 1) * width] = terms.astype(BF16)

    def send(i, _):
        for u in range(2):
            p = 2 * i + u
            part = jnp.dot(terms_v[...], choose_v[p], preferred_element_type=F32).astype(BF16)
            out_v[2 * p] = part[:, :cap]
            out_v[2 * p + 1] = part[:, cap:]
        return 0

    lax.fori_loop(0, pairs // 2, send, 0, unroll=True)


def layer(got, first, code, w1_self, w1_neigh, bias1, w2, fanout):
    blocks, _, cap = got.shape
    rest, slots, width = code.shape
    nodes = (rest + 1) * width
    return pl.pallas_call(
        functools.partial(layer_kernel, fanout),
        out_shape=pltpu.HBM((blocks, w2.shape[0], cap), BF16),
        in_specs=[WHOLE_VMEM, WHOLE_VMEM, IN_HBM] + [WHOLE_VMEM] * 4,
        out_specs=WHOLE_VMEM,
        scratch_shapes=[
            pltpu.VMEM(code.shape, BF16),
            pltpu.VMEM((w1_self.shape[1], slots), BF16),
            pltpu.VMEM((blocks // 2, nodes, 2 * cap), BF16),
            pltpu.VMEM((w2.shape[0], nodes), BF16),
            pltpu.SemaphoreType.DMA((rest,)),
        ],
        compiler_params=params(40),
        name="layer",
    )(got, first, pltpu.with_memory_space_constraint(code, pltpu.HBM), w1_self, w1_neigh, bias1[:, None], w2)


def wide(ref, first, last, lo, hi):
    return jnp.concatenate([ref[o, lo:hi] for o in range(first, last)], axis=1)


def logits_kernel(fanout, got_ref, code_ref, b_ref, out_ref):
    blocks, half = got_ref.shape[0], got_ref.shape[1] // 2
    classes = out_ref.shape[0]
    own_w = own_weight(fanout)
    code = code_ref[0]
    own = split_codes(code, own_w)
    mine = jnp.dot(wide(got_ref, 0, blocks, 0, half), own, preferred_element_type=F32)
    near = jnp.dot(wide(got_ref, 0, blocks, half, 2 * half), code - own_w * own, preferred_element_type=F32) / fanout
    out_ref[...] = (mine + near)[:classes] + b_ref[...]


def final(got, code, bias2, fanout):
    return pl.pallas_call(
        functools.partial(logits_kernel, fanout),
        out_shape=jax.ShapeDtypeStruct((bias2.shape[0], code.shape[2]), F32),
        in_specs=[WHOLE_VMEM] * 3,
        out_specs=WHOLE_VMEM,
        compiler_params=params(20),
        name="logits",
    )(got, code, bias2[:, None])


def mask_rows(received, counts, capacity):
    is_live = (jnp.arange(capacity, dtype=jnp.int32)[None, :] < counts[:, None]).reshape(-1)
    flat = received.reshape(-1, received.shape[-1])
    return jnp.where(is_live[:, None], flat, jnp.zeros((), flat.dtype))


def right_product(rows, weight):
    return lax.dot_general(
        rows, weight, (((1,), (1,)), ((), ())), preferred_element_type=jnp.float32
    )


def plain_body(
    table_t,
    req_rows,
    count1,
    frontier_list,
    req2_rows,
    count2,
    seed_list,
    w1_self,
    w1_neigh,
    bias1,
    w2_self,
    w2_neigh,
    bias2,
):
    feat_width = table_t.shape[0]
    capacity = req_rows.shape[1]
    table_rows = table_t.T
    picked_rows = jnp.take(
        table_rows,
        lax.all_to_all(req_rows, AXES, split_axis=0, concat_axis=0, tiled=True),
        axis=0,
    )
    received = lax.all_to_all(
        picked_rows, AXES, split_axis=0, concat_axis=0, tiled=True
    )
    flat = mask_rows(received, count1, capacity)
    fanout_two = frontier_list.shape[0] - 1
    front_nodes = frontier_list.shape[1]
    picked = jnp.take(flat, frontier_list.reshape(-1), axis=0).reshape(
        fanout_two + 1, front_nodes, feat_width
    )
    summed = (jnp.sum(picked[1:].astype(jnp.float32), axis=0) / fanout_two).astype(jnp.bfloat16)
    preact = right_product(picked[0], w1_self) + right_product(summed, w1_neigh) + bias1[None, :]
    hidden_rows = jax.nn.relu(preact).astype(jnp.bfloat16)
    cap_two = req2_rows.shape[1]
    payload = jnp.concatenate(
        [right_product(hidden_rows, w2_self), right_product(hidden_rows, w2_neigh)], axis=1
    )
    chosen = jnp.take(
        payload,
        lax.all_to_all(req2_rows, AXES, split_axis=0, concat_axis=0, tiled=True),
        axis=0,
    )
    got_back = lax.all_to_all(chosen, AXES, split_axis=0, concat_axis=0, tiled=True)
    flat_two = mask_rows(got_back, count2, cap_two)
    fanout_one = seed_list.shape[0] - 1
    seed_nodes = seed_list.shape[1]
    picked_two = jnp.take(flat_two, seed_list.reshape(-1), axis=0).reshape(
        fanout_one + 1, seed_nodes, flat_two.shape[1]
    )
    classes = w2_self.shape[0]
    near = jnp.sum(picked_two[1:, :, classes:], axis=0) / fanout_one
    logits = (picked_two[0, :, :classes] + near).T + bias2[:, None]
    return logits


MOST = 8 << 20


def body(
    table_t,
    req_rows,
    count1,
    frontier_list,
    req2_rows,
    count2,
    seed_list,
    w1_self,
    w1_neigh,
    bias1,
    w2_self,
    w2_neigh,
    bias2,
):
    cap = req_rows.shape[1]
    fits = req_rows.size * frontier_list.shape[1] <= MOST and req2_rows.shape[1] == cap
    if not fits or table_t.shape[1] > 32768 or frontier_list.shape[1] > 65536:
        return plain_body(
            table_t,
            req_rows,
            count1,
            frontier_list,
            req2_rows,
            count2,
            seed_list,
            w1_self,
            w1_neigh,
            bias1,
            w2_self,
            w2_neigh,
            bias2,
        )
    idx = exchange(req_rows)
    got1 = exchange(fetch(idx, req2_rows, table_t))
    first = codes(count1, frontier_list[:, :256], cap, jax.ShapeDtypeStruct)
    code1 = codes(count1, frontier_list[:, 256:], cap, pltpu.HBM)
    classes = w2_self.shape[0]
    half = -(-classes // 16) * 16
    pad = ((0, half - classes), (0, 0))
    w2 = jnp.concatenate([jnp.pad(w2_self, pad), jnp.pad(w2_neigh, pad)], axis=0)
    out2 = layer(got1, first, code1, w1_self, w1_neigh, bias1, w2, frontier_list.shape[0] - 1)
    got2 = exchange(out2)
    code2 = codes(count2, seed_list, cap, jax.ShapeDtypeStruct)
    return final(got2, code2, bias2, seed_list.shape[0] - 1)


def solution(mesh):
    split, split1 = P(AXES, None), P(AXES)
    cols = P(None, AXES)
    in_specs = (cols, split, split1, cols, split, split1, cols, P(), P(), P(), P(), P(), P())
    return jax.shard_map(body, mesh=mesh, in_specs=in_specs, out_specs=cols, check_vma=False)
```

time: 98.1 us -> 80.5 us (0.82)
  blocking collectives: 0 us -> 14.4 us
  Pallas kernels: 48.6 us -> 35.7 us
  local copies, waits for them, and re-layouts: 13 us -> 0.54 us
  starting transfers between devices: 18.6 us -> 6.2 us
  waiting for transfers between devices: 15.8 us -> 23.1 us
  other arithmetic: 1.35 us -> 0.01 us
    all_to_all x0 -> x1, blocking collectives: none -> 14.4 us  [exchange(): return lax.all_to_all(blocks, AXES, split_axis=0, concat_axis=0, tiled=True)]
    pallas_call x5, Pallas kernels: 47.1 us -> 34.2 us  [the longest x3 18.8 us: codes(): pl.pallas_call(functools.partial(codes_kernel, own_weight(depth - 1), cap...]
    all_to_all x3 -> x2, starting transfers between devices: 18.6 us -> 6.2 us  [exchange(): return lax.all_to_all(blocks, AXES, split_axis=0, concat_axis=0, tiled=True)]
    all_to_all x3 -> x2, waiting for transfers between devices: 15.8 us -> 23.1 us  [exchange(): return lax.all_to_all(blocks, AXES, split_axis=0, concat_axis=0, tiled=True)]
    transpose x1 -> x0, local copies, waits for them, and re-layouts: 6.68 us -> none  [fetch(): pairs = table_t.T.reshape(n // 2, 2, feats)]
    unnamed x26 -> x22, local copies, waits for them, and re-layouts: 6.08 us -> 0.3 us
    add x1 -> x0, other arithmetic: 1.34 us -> none  [body(): asked = exchange(req_rows * 65536 + req2_rows)]
  transfers between devices with their start and end apart: 3 -> 2, of which waited for: 2 -> 2; matrix products, arithmetic and copies ran while one was open for 7% -> 1% of each run, Pallas kernels for 29% -> 23%
where the time goes in v2:
time: 80.5 us; the launch traced here: 80.2 us
  Pallas kernels  35.7 us (44%)
  waiting for transfers between devices  23.1 us (29%)
  blocking collectives  14.4 us (18%)
  starting transfers between devices  6.2 us (8%)
    all_to_all x2, waiting for transfers between devices, exchange(): return lax.all_to_all(blocks, AXES, split_axis=0, concat_axis=0, tiled=True)  23.1 us
    pallas_call x3, Pallas kernels, codes(): pl.pallas_call(functools.partial(codes_kernel, own_weight(depth - 1), cap...  18.8 us
    all_to_all x1, blocking collectives, exchange(): return lax.all_to_all(blocks, AXES, split_axis=0, concat_axis=0, tiled=True)  14.4 us
    pallas_call x1, Pallas kernels, layer(): pl.pallas_call(functools.partial(layer_kernel, fanout), out_shape=pltpu.H...  8.08 us
    pallas_call x1, Pallas kernels, fetch(): pl.pallas_call(functools.partial(fetch_kernel, parts, parts, group), out_...  7.42 us
    all_to_all x2, starting transfers between devices, exchange(): return lax.all_to_all(blocks, AXES, split_axis=0, concat_axis=0, tiled=True)  6.2 us
  transfers between devices with their start and end apart: 2, of which 2 were waited for; matrix products, arithmetic and copies ran while one was open for 1% of the time, Pallas kernels for 23%

profile of v2, /device:TPU:0, one launch (start us, length us, event | category | flops | bytes accessed | tf_op | source)
XLA Modules:
  0.0 80.2 jit_solution(271453804155257506)
XLA Ops:
  0.0 14.4 %all_to_all.21 = s32[32,1,128]{2,1,0:T(1,128)S(1)} all-to-all(s32[32,1,128]{2,1,0:T(1,128)} %bitcast.5), channel_id=1, replica_groups=mesh['shard'=8,'grp'=4] {'shard','grp'}, dimensions={0} | all-to-all | bytes 32768 | tf_op jit(solution)/shard_map/all_to_all | solution.py:20
  14.4 7.4 %fetch.1 = bf16[32,102,128]{2,1,0:T(8,128)(2,1)} custom-call(s32[32,128]{1,0:T(8,128)S(1)} %bitcast.4, s32[32,128]{1,0:T(8,128)} %asked_hbm.1, bf16[100,19456]{1,0:T(8,128)(2,1)} %table_hbm.1), custom_call_target="tpu_custom_call" | custom-call | tf_op jit(solution)/shard_map/fetch/pallas_call | solution.py:116
  21.9 2.6 %all-to-all-start.1 = ((bf16[32,102,128]{2,1,0:T(8,128)(2,1)}), bf16[32,102,128]{2,1,0:T(8,128)(2,1)S(1)}, u32[]{:S(2)}, u32[]{:S(2)}) async-start(bf16[32,102,128]{2,1,0:T(8,128)(2,1)} %fetch.1), calls=%async_computation.1 | async-start | bytes 1703936 | tf_op jit(solution)/shard_map/all_to_all | solution.py:20
  24.6 0.0 copy-start.8
  24.6 0.0 copy-start.4
  24.6 0.0 copy-start.5
  24.6 0.0 copy-start.6
  24.6 0.0 copy-start.7
  24.6 10.6 %codes.4.codes_hbm = bf16[3,4096,256]{2,1,0:T(8,128)(2,1)} custom-call(s32[32]{0:T(128)S(1)} %copy-done.1, s32[11,768]{1,0:T(8,128)S(1)} %slice.7.list_ref), custom_call_target="tpu_custom_call" | custom-call | tf_op jit(solution)/shard_map/codes/pallas_call | solution.py:170
  35.2 3.5 %codes.3.first_ref = bf16[1,4096,256]{2,1,0:T(8,128)(2,1)S(1)} custom-call(s32[32]{0:T(128)S(1)} %copy-done.1, s32[11,256]{1,0:T(8,128)S(1)} %slice.6.list_ref), custom_call_target="tpu_custom_call" | custom-call | tf_op jit(solution)/shard_map/codes/pallas_call | solution.py:170
  38.7 0.1 copy.23.b_ref
  38.9 0.1 copy.21.ws_ref
  39.0 0.1 copy.22.wn_ref
  39.1 0.0 copy-done.6
  39.2 0.0 copy-start.9
  39.2 0.0 copy-start
  39.2 0.0 copy-start.2
  39.2 7.3 %all-to-all-done.1.got_ref = bf16[32,102,128]{2,1,0:T(8,128)(2,1)S(1)} async-done(((bf16[32,102,128]{2,1,0:T(8,128)(2,1)}), bf16[32,102,128]{2,1,0:T(8,128)(2,1)S(1)}, u32[]{:S(2)}, u32[]{:S(2)}) %all-to-all-start.1) | async-done | bytes 835616 | tf_op jit(solution)/shard_map/all_to_all | solution.py:20
  46.5 8.1 %layer.1 = bf16[32,96,128]{2,1,0:T(8,128)(2,1)} custom-call(bf16[32,102,128]{2,1,0:T(8,128)(2,1)S(1)} %all-to-all-done.1.got_ref, bf16[1,4096,256]{2,1,0:T(8,128)(2,1)S(1)} %codes.3.first_ref, bf16[3,4096,256]{2,1,0:T(8,128)(2,1)} %codes.4.codes_hbm, bf16[256,100]{1,0:T(8,128)(2,1)S(1)} %copy.21.ws_ref, bf16[256,100]{1,0:T(8,128)(2,1)S(1)} %copy.22.wn_ref, ...), custom_call_target="tpu_custom_call" | custom-call | tf_op jit(solution)/shard_map/layer/pallas_call | solution.py:245
  54.6 3.5 %all-to-all-start.2 = ((bf16[32,96,128]{2,1,0:T(8,128)(2,1)}), bf16[32,96,128]{2,1,0:T(8,128)(2,1)S(1)}, u32[]{:S(2)}, u32[]{:S(2)}) async-start(bf16[32,96,128]{2,1,0:T(8,128)(2,1)} %layer.1), calls=%async_computation.2 | async-start | bytes 1572864 | tf_op jit(solution)/shard_map/all_to_all | solution.py:20
  58.1 0.1 copy.24.b_ref
  58.3 4.7 %codes.5.code_ref = bf16[1,4096,256]{2,1,0:T(8,128)(2,1)S(1)} custom-call(s32[32]{0:T(128)S(1)} %copy-done.2, s32[16,256]{1,0:T(8,128)S(1)} %copy-done), custom_call_target="tpu_custom_call" | custom-call | tf_op jit(solution)/shard_map/codes/pallas_call | solution.py:170
  63.0 15.8 %all-to-all-done.2.got_ref = bf16[32,96,128]{2,1,0:T(8,128)(2,1)S(1)} async-done(((bf16[32,96,128]{2,1,0:T(8,128)(2,1)}), bf16[32,96,128]{2,1,0:T(8,128)(2,1)S(1)}, u32[]{:S(2)}, u32[]{:S(2)}) %all-to-all-start.2) | async-done | bytes 786464 | tf_op jit(solution)/shard_map/all_to_all | solution.py:20
  78.7 1.5 %logits.1 = f32[47,256]{1,0:T(8,128)} custom-call(bf16[32,96,128]{2,1,0:T(8,128)(2,1)S(1)} %all-to-all-done.2.got_ref, bf16[1,4096,256]{2,1,0:T(8,128)(2,1)S(1)} %codes.5.code_ref, f32[47,1]{1,0:T(8,128)S(1)} %copy.24.b_ref), custom_call_target="tpu_custom_call" | custom-call | tf_op jit(solution)/shard_map/logits/pallas_call | solution.py:278
  (14 shorter events, 0.0 us)
Async XLA Ops:
  0.0 24.5 %copy-start.3 = (s32[11,1024]{1,0:T(8,128)S(1)}, s32[11,1024]{1,0:T(8,128)}, u32[]{:S(2)}) copy-start(s32[11,1024]{1,0:T(8,128)} %param.16) | copy-start | bytes 135172
  0.0 24.6 %copy-start.1 = (s32[32]{0:T(128)S(1)}, s32[32]{0:T(128)}, u32[]{:S(2)}) copy-start(s32[32]{0:T(128)} %count_ref.4) | copy-start | bytes 388
  21.9 24.6 %all-to-all-start.1 = ((bf16[32,102,128]{2,1,0:T(8,128)(2,1)}), bf16[32,102,128]{2,1,0:T(8,128)(2,1)S(1)}, u32[]{:S(2)}, u32[]{:S(2)}) async-start(bf16[32,102,128]{2,1,0:T(8,128)(2,1)} %fetch.1), calls=%async_computation.1 | async-start | bytes 1703936 | tf_op jit(solution)/shard_map/all_to_all | solution.py:20
  24.6 14.1 %copy-start.8 = (f32[256]{0:T(256)S(1)}, f32[256]{0:T(256)}, u32[]{:S(2)}) copy-start(f32[256]{0:T(256)} %param.22) | copy-start | bytes 3076
  24.6 14.3 %copy-start.4 = (bf16[256,100]{0,1:T(8,128)(2,1)S(1)}, bf16[256,100]{0,1:T(8,128)(2,1)}, u32[]{:S(2)}) copy-start(bf16[256,100]{0,1:T(8,128)(2,1)} %param.20) | copy-start | bytes 153604
  24.6 14.4 %copy-start.5 = (bf16[256,100]{0,1:T(8,128)(2,1)S(1)}, bf16[256,100]{0,1:T(8,128)(2,1)}, u32[]{:S(2)}) copy-start(bf16[256,100]{0,1:T(8,128)(2,1)} %param.21) | copy-start | bytes 153604
  24.6 14.5 %copy-start.6 = (bf16[47,256]{1,0:T(8,128)(2,1)S(1)}, bf16[47,256]{1,0:T(8,128)(2,1)}, u32[]{:S(2)}) copy-start(bf16[47,256]{1,0:T(8,128)(2,1)} %param.24) | copy-start | bytes 72196
  24.6 14.5 %copy-start.7 = (bf16[47,256]{1,0:T(8,128)(2,1)S(1)}, bf16[47,256]{1,0:T(8,128)(2,1)}, u32[]{:S(2)}) copy-start(bf16[47,256]{1,0:T(8,128)(2,1)} %param.23) | copy-start | bytes 72196
  39.2 19.0 %copy-start.9 = (f32[47]{0:T(128)S(1)}, f32[47]{0:T(128)}, u32[]{:S(2)}) copy-start(f32[47]{0:T(128)} %param.25) | copy-start | bytes 568
  39.2 19.1 %copy-start = (s32[16,256]{1,0:T(8,128)S(1)}, s32[16,256]{1,0:T(8,128)}, u32[]{:S(2)}) copy-start(s32[16,256]{1,0:T(8,128)} %list_ref.1) | copy-start | bytes 49156
  39.2 19.1 %copy-start.2 = (s32[32]{0:T(128)S(1)}, s32[32]{0:T(128)}, u32[]{:S(2)}) copy-start(s32[32]{0:T(128)} %count_ref.5) | copy-start | bytes 388
  54.6 24.1 %all-to-all-start.2 = ((bf16[32,96,128]{2,1,0:T(8,128)(2,1)}), bf16[32,96,128]{2,1,0:T(8,128)(2,1)S(1)}, u32[]{:S(2)}, u32[]{:S(2)}) async-start(bf16[32,96,128]{2,1,0:T(8,128)(2,1)} %layer.1), calls=%async_computation.2 | async-start | bytes 1572864 | tf_op jit(solution)/shard_map/all_to_all | solution.py:20

commit v3 on v2

--- a/solution.py
+++ b/solution.py
@@ -31,7 +31,7 @@
 
 
 def fetch_kernel(
-    parts, ahead, group, idx_ref, asked_hbm, table_hbm, out_hbm, cols, rows, even, odd, slots, out_v, asked_v, sems, out_sems, slot_sems
+    parts, ahead, group, idx_ref, extra_hbm, table_hbm, out_hbm, cols, rows, even, odd, slots, out_v, extra_v, sems, out_sems, slot_sems
 ):
     feats, n = cols.shape
     blocks, rows_out, cap = out_v.shape
@@ -50,7 +50,7 @@
 
     refill(0, 0).start()
     refill(1, group).start()
-    ask = pltpu.make_async_copy(asked_hbm, asked_v, sems.at[parts])
+    ask = pltpu.make_async_copy(extra_hbm, extra_v, sems.at[parts])
     ask.start()
     wide = max(w for w in range(1, 9) if (span // 128) % w == 0)
     for i in range(parts):
@@ -67,8 +67,8 @@
         lax.fori_loop(0, span // 128 // wide, tile, 0, unroll=True)
 
     ask.wait()
-    base = feats // 16 * 16
-    row = lax.broadcasted_iota(I32, (16, cap), 0)
+    base = feats // 8 * 8
+    row = lax.broadcasted_iota(I32, (8, cap), 0)
 
     def gather(slot, u, buf):
         for j in range(cap):
@@ -76,11 +76,8 @@
 
     def turn(r, buf):
         y = buf[...].T
-        asked = asked_v[pl.ds(r, 1), :]
-        high, low = (asked // cap).astype(F32), (asked % cap).astype(F32)
-        tail = jnp.where(row == feats - base, high, jnp.where(row == feats - base + 1, low, y[base : base + 16]))
         out_v[r, :base] = y[:base].astype(BF16)
-        out_v[r, base:] = tail[: rows_out - base].astype(BF16)
+        out_v[r, base:] = jnp.where(row < feats - base, y[base : base + 8], extra_v[r]).astype(BF16)
 
     def leave(i):
         return pltpu.make_async_copy(out_v.at[pl.ds(i * group, group)], out_hbm.at[pl.ds(i * group, group)], out_sems.at[i])
@@ -108,14 +105,14 @@
         leave(i).wait()
 
 
-def fetch(idx, asked, table_t):
+def fetch(idx, extra, table_t):
     feats, n = table_t.shape
     blocks, cap = idx.shape
     parts = 8 if n % 1024 == 0 else 1
     group = 4
     return pl.pallas_call(
         functools.partial(fetch_kernel, parts, parts, group),
-        out_shape=pltpu.HBM((blocks, feats + 2, cap), BF16),
+        out_shape=pltpu.HBM((blocks, feats + 4, cap), BF16),
         in_specs=[WHOLE_VMEM, IN_HBM, IN_HBM],
         out_specs=IN_HBM,
         scratch_shapes=[
@@ -124,15 +121,73 @@
             pltpu.VMEM((cap, 128), F32),
             pltpu.VMEM((cap, 128), F32),
             [pltpu.SMEM((group, cap), I32), pltpu.SMEM((group, cap), I32)],
-            pltpu.VMEM((blocks, feats + 2, cap), BF16),
-            pltpu.VMEM((blocks, cap), I32),
+            pltpu.VMEM((blocks, feats + 4, cap), BF16),
+            pltpu.VMEM((blocks, 8, cap), F32),
             pltpu.SemaphoreType.DMA((parts + 1,)),
             pltpu.SemaphoreType.DMA((blocks // group,)),
             pltpu.SemaphoreType.DMA((2,)),
         ],
         compiler_params=params(40),
         name="fetch",
-    )(idx, pltpu.with_memory_space_constraint(asked, pltpu.HBM), pltpu.with_memory_space_constraint(table_t, pltpu.HBM))
+    )(idx, pltpu.with_memory_space_constraint(extra, pltpu.HBM), pltpu.with_memory_space_constraint(table_t, pltpu.HBM))
+
+
+PARTS = 6
+
+
+def room_of(cap):
+    return cap // PARTS
+
+
+def lane_part(shape, cap):
+    lane = lax.broadcasted_iota(I32, shape, len(shape) - 1)
+    part = lane // room_of(cap)
+    return jnp.where(part < PARTS, part, -1), lane % room_of(cap)
+
+
+def ask_kernel(off, req2_ref, seeds_ref, extra_ref, rank_ref):
+    blocks, cap = req2_ref.shape
+    own = seeds_ref[0:1, :]
+    seeds = own.shape[1]
+    room = room_of(cap)
+    owner, slot = own // cap, own % cap
+
+    def bits(mask):
+        return jnp.where(mask, 1.0, 0.0).astype(BF16)
+
+    mine = bits(lax.broadcasted_iota(I32, (blocks, seeds), 0) == owner)
+    before = bits(lax.broadcasted_iota(I32, (seeds, seeds), 0) < lax.broadcasted_iota(I32, (seeds, seeds), 1))
+    mine32 = mine.astype(F32)
+    rank = jnp.sum(mine32 * jnp.dot(mine, before, preferred_element_type=F32), axis=0, keepdims=True)
+    rank_ref[...] = rank
+    at_slot = bits(lax.broadcasted_iota(I32, (cap, seeds), 0) == slot)
+    lane = lax.broadcasted_iota(I32, (cap, seeds), 0)
+    entry = jnp.where(lane // room < PARTS, lane % room, -1).astype(F32)
+    at_rank = bits(entry == rank)
+    full = jnp.max(jnp.where(rank >= room, 1.0, 0.0))
+    last = lax.broadcasted_iota(I32, (blocks, cap), 1) == cap - 1
+    extra_ref[...] = jnp.zeros_like(extra_ref)
+    for k, part in enumerate((req2_ref[...] // cap, req2_ref[...] % cap)):
+        part = part.astype(F32)
+        extra_ref[:, off + k, :] = part
+        node = jnp.dot(part.astype(BF16), at_slot, preferred_element_type=F32) * mine32
+        listed = lax.dot_general(node.astype(BF16), at_rank, (((1,), (1,)), ((), ())), preferred_element_type=F32)
+        extra_ref[:, off + 2 + k, :] = jnp.where(last, full, listed)
+
+
+def ask(req2_rows, seed_list, feats):
+    blocks, cap = req2_rows.shape
+    return pl.pallas_call(
+        functools.partial(ask_kernel, feats % 8),
+        out_shape=(
+            jax.ShapeDtypeStruct((blocks, 8, cap), F32),
+            jax.ShapeDtypeStruct((1, seed_list.shape[1]), F32),
+        ),
+        in_specs=[WHOLE_VMEM, WHOLE_VMEM],
+        out_specs=(WHOLE_VMEM, WHOLE_VMEM),
+        compiler_params=params(8),
+        name="ask",
+    )(req2_rows, seed_list)
 
 
 def own_weight(fanout):
@@ -178,18 +233,62 @@
     )(counts, lists)
 
 
+def rank_codes_kernel(own, cap, count_ref, list_ref, rank_ref, out_ref):
+    depth, width = list_ref.shape
+    each = out_ref.shape[0] // cap
+    zero = jnp.zeros((16, width), BF16)
+    hit = [jnp.full((16, width), v, BF16) for v in (own, 1)]
+
+    def step(t, _):
+        o = pl.program_id(0) * each + t
+        local = list_ref[...] - o * cap
+        live = (local >= 0) & (local < count_ref[o])
+        local = jnp.where(live, local, -1).astype(F32)
+        rank = jnp.where(live[0:1], rank_ref[...], -cap * 1.0)
+        rank = jnp.where(rank < room_of(cap), rank, -cap * 1.0)
+        rows = [rank + q * room_of(cap) for q in range(PARTS)] + [local[k : k + 1] for k in range(1, depth)]
+        want = [jnp.broadcast_to(row, (16, width)).astype(BF16) for row in rows]
+        for g in range(cap // 16):
+            slot = (lax.broadcasted_iota(I32, (16, width), 0) + g * 16).astype(F32).astype(BF16)
+            total = jnp.where(want[0] == slot, hit[0], zero)
+            for k in range(1, len(rows)):
+                total = total + jnp.where(want[k] == slot, hit[k >= PARTS], zero)
+            out_ref[pl.ds(pl.multiple_of(t * cap + g * 16, 16), 16), :] = total
+        return 0
+
+    lax.fori_loop(0, each, step, 0)
+
+
+def rank_codes(counts, lists, rank, cap):
+    depth, seeds = lists.shape
+    blocks = counts.shape[0]
+    each = 8
+    return pl.pallas_call(
+        functools.partial(rank_codes_kernel, own_weight(depth - 1), cap),
+        grid=(blocks // each,),
+        out_shape=jax.ShapeDtypeStruct((blocks * cap, seeds), BF16),
+        in_specs=[WHOLE_SMEM, WHOLE_VMEM, WHOLE_VMEM],
+        out_specs=pl.BlockSpec((each * cap, seeds), lambda o: (o, 0)),
+        compiler_params=params(8),
+        name="rank_codes",
+    )(counts, lists, rank)
+
+
 def split_codes(code, own):
     return jnp.where(code >= own, jnp.ones((), BF16), jnp.zeros((), BF16))
 
 
 def layer_kernel(
-    fanout, got_ref, first_ref, codes_hbm, ws_ref, wn_ref, b_ref, w2_ref, out_v, codes_v, got_v, choose_v, terms_v, sems
+    fanout, got_ref, first_ref, codes_hbm, ws_ref, wn_ref, b_ref, w2_ref, out_v, terms_ref, flag_ref, codes_v, got_v, choose_v, terms_v, sems
 ):
     blocks, _, cap = got_ref.shape
     feats = got_v.shape[0]
     rest, slots, width = codes_v.shape
     parts = rest + 1
-    pairs, nodes, _ = choose_v.shape
+    pairs, nodes = blocks // 2, choose_v.shape[1]
+    chunks = -(-blocks // PARTS)
+    half = w2_ref.shape[0] // 2
+    deep = half // PARTS
     own_w = own_weight(fanout)
     def load(q):
         return pltpu.make_async_copy(codes_hbm.at[q], codes_v.at[q], sems.at[q])
@@ -197,23 +296,38 @@
     for q in range(rest):
         load(q).start()
     one, zero = jnp.ones((16, cap), BF16), jnp.zeros((16, cap), BF16)
+
+    def fill(asked, p, u):
+        for base in range(0, nodes, 256):
+            local = asked - base
+            local = jnp.where((local >= 0) & (local < 256), local, -1.0)
+            want = jnp.broadcast_to(local, (16, cap)).astype(BF16)
+            for g in range(0, 256, 16):
+                node = (lax.broadcasted_iota(I32, (16, cap), 0) + g).astype(F32).astype(BF16)
+                choose_v[p, base + g : base + g + 16, u * cap : (u + 1) * cap] = jnp.where(want == node, one, zero)
+
+    def asked_of(o, row):
+        asked = got_ref[o, feats : feats + 4].astype(F32)
+        return asked[row : row + 1] * cap + asked[row + 1 : row + 2]
 
     def choose(p, _):
         for u in range(2):
             o = 2 * p + u
             got_v[:, pl.ds(pl.multiple_of(o * cap, cap), cap)] = got_ref[o, :feats]
-            asked = got_ref[o, feats : feats + 2].astype(F32)
-            asked = asked[0:1] * cap + asked[1:2]
-            for base in range(0, nodes, 256):
-                local = asked - base
-                local = jnp.where((local >= 0) & (local < 256), local, -1.0)
-                want = jnp.broadcast_to(local, (16, cap)).astype(BF16)
-                for g in range(0, 256, 16):
-                    node = (lax.broadcasted_iota(I32, (16, cap), 0) + g).astype(F32).astype(BF16)
-                    choose_v[p, base + g : base + g + 16, u * cap : (u + 1) * cap] = jnp.where(want == node, one, zero)
+            fill(asked_of(o, 0), p, u)
         return 0
 
     lax.fori_loop(0, pairs, choose, 0)
+    part, _ = lane_part((1, cap), cap)
+    for c in range(chunks):
+        asked = jnp.full((1, cap), -1.0, F32)
+        for u in range(min(PARTS, blocks - c * PARTS)):
+            asked = jnp.where(part == u, asked_of(c * PARTS + u, 2), asked)
+        fill(asked, pairs + c // 2, c % 2)
+    flag = got_ref[0, feats + 2 : feats + 3].astype(F32)
+    for o in range(1, blocks):
+        flag = jnp.maximum(flag, got_ref[o, feats + 2 : feats + 3].astype(F32))
+    flag_ref[...] = flag
     for q in range(parts):
         if q:
             load(q - 1).wait()
@@ -227,30 +341,43 @@
         terms = jnp.dot(w2_ref[...], hidden, preferred_element_type=F32)
         terms_v[:, q * width : (q + 1) * width] = terms.astype(BF16)
 
-    def send(i, _):
-        for u in range(2):
-            p = 2 * i + u
-            part = jnp.dot(terms_v[...], choose_v[p], preferred_element_type=F32).astype(BF16)
-            out_v[2 * p] = part[:, :cap]
-            out_v[2 * p + 1] = part[:, cap:]
-        return 0
-
-    lax.fori_loop(0, pairs // 2, send, 0, unroll=True)
+    terms_ref[...] = terms_v[:half]
+    part8, _ = lane_part((deep, cap), cap)
+    for p in range(pairs, choose_v.shape[0]):
+        found = jnp.dot(terms_v[:half], choose_v[p], preferred_element_type=F32)
+        for v in range(2):
+            c = 2 * (p - pairs) + v
+            for u in range(max(0, min(PARTS, blocks - c * PARTS))):
+                block = jnp.zeros((deep, cap), F32)
+                for q in range(PARTS):
+                    piece = found[q * deep : (q + 1) * deep, v * cap : (v + 1) * cap]
+                    piece = pltpu.roll(piece, (q - u) * room_of(cap) % cap, 1)
+                    block = jnp.where(part8 == q, piece, block)
+                out_v[c * PARTS + u, half:] = block.astype(BF16)
+    for p in range(pairs):
+        near = jnp.dot(terms_v[half:], choose_v[p], preferred_element_type=F32).astype(BF16)
+        out_v[2 * p, :half] = near[:, :cap]
+        out_v[2 * p + 1, :half] = near[:, cap:]
 
 
 def layer(got, first, code, w1_self, w1_neigh, bias1, w2, fanout):
     blocks, _, cap = got.shape
     rest, slots, width = code.shape
     nodes = (rest + 1) * width
+    half = w2.shape[0] // 2
     return pl.pallas_call(
         functools.partial(layer_kernel, fanout),
-        out_shape=pltpu.HBM((blocks, w2.shape[0], cap), BF16),
+        out_shape=(
+            pltpu.HBM((blocks, half + half // PARTS, cap), BF16),
+            pltpu.HBM((half, nodes), BF16),
+            jax.ShapeDtypeStruct((1, cap), F32),
+        ),
         in_specs=[WHOLE_VMEM, WHOLE_VMEM, IN_HBM] + [WHOLE_VMEM] * 4,
-        out_specs=WHOLE_VMEM,
+        out_specs=(WHOLE_VMEM,) * 3,
         scratch_shapes=[
             pltpu.VMEM(code.shape, BF16),
             pltpu.VMEM((w1_self.shape[1], slots), BF16),
-            pltpu.VMEM((blocks // 2, nodes, 2 * cap), BF16),
+            pltpu.VMEM((blocks // 2 + -(-blocks // (2 * PARTS)), nodes, 2 * cap), BF16),
             pltpu.VMEM((w2.shape[0], nodes), BF16),
             pltpu.SemaphoreType.DMA((rest,)),
         ],
@@ -354,6 +481,35 @@
     return logits
 
 
+def rank_logits_kernel(fanout, got_ref, code_ref, b_ref, out_ref):
+    blocks, rows, cap = got_ref.shape
+    deep = rows // (PARTS + 1)
+    half = rows - deep
+    own_w = own_weight(fanout)
+    code = code_ref[...]
+    own = split_codes(code, own_w)
+    part, _ = lane_part((deep, cap), cap)
+
+    def spread(o):
+        terms = got_ref[o, half:].astype(F32)
+        return jnp.concatenate([jnp.where(part == q, terms, 0.0) for q in range(PARTS)], axis=0).astype(BF16)
+
+    mine = jnp.dot(jnp.concatenate([spread(o) for o in range(blocks)], axis=1), own, preferred_element_type=F32)
+    near = jnp.dot(wide(got_ref, 0, blocks, 0, half), code - own_w * own, preferred_element_type=F32) / fanout
+    out_ref[...] = (mine + near)[: out_ref.shape[0]] + b_ref[...]
+
+
+def rank_final(got, code, bias2, fanout):
+    return pl.pallas_call(
+        functools.partial(rank_logits_kernel, fanout),
+        out_shape=pltpu.HBM((bias2.shape[0], code.shape[1]), F32),
+        in_specs=[WHOLE_VMEM] * 3,
+        out_specs=WHOLE_VMEM,
+        compiler_params=params(20),
+        name="rank_logits",
+    )(got, code, bias2[:, None])
+
+
 MOST = 8 << 20
 
 
@@ -373,7 +529,7 @@
     bias2,
 ):
     cap = req_rows.shape[1]
-    fits = req_rows.size * frontier_list.shape[1] <= MOST and req2_rows.shape[1] == cap
+    fits = req_rows.size * frontier_list.shape[1] <= MOST and req2_rows.shape[1] == cap and table_t.shape[0] % 8 == 4
     if not fits or table_t.shape[1] > 32768 or frontier_list.shape[1] > 65536:
         return plain_body(
             table_t,
@@ -390,18 +546,26 @@
             w2_neigh,
             bias2,
         )
-    idx = exchange(req_rows)
-    got1 = exchange(fetch(idx, req2_rows, table_t))
+    feats, fanout_two, fanout_one = table_t.shape[0], frontier_list.shape[0] - 1, seed_list.shape[0] - 1
+    extra, rank = ask(req2_rows, seed_list, feats)
+    got1 = exchange(fetch(exchange(req_rows), extra, table_t))
     first = codes(count1, frontier_list[:, :256], cap, jax.ShapeDtypeStruct)
     code1 = codes(count1, frontier_list[:, 256:], cap, pltpu.HBM)
     classes = w2_self.shape[0]
-    half = -(-classes // 16) * 16
+    half = -(-classes // 48) * 48
     pad = ((0, half - classes), (0, 0))
     w2 = jnp.concatenate([jnp.pad(w2_self, pad), jnp.pad(w2_neigh, pad)], axis=0)
-    out2 = layer(got1, first, code1, w1_self, w1_neigh, bias1, w2, frontier_list.shape[0] - 1)
+    out2, terms, flag = layer(got1, first, code1, w1_self, w1_neigh, bias1, w2, fanout_two)
     got2 = exchange(out2)
-    code2 = codes(count2, seed_list, cap, jax.ShapeDtypeStruct)
-    return final(got2, code2, bias2, seed_list.shape[0] - 1)
+    logits = rank_final(got2, rank_codes(count2, seed_list, rank, cap), bias2, fanout_one)
+
+    def in_full(logits):
+        asked = exchange(req2_rows)
+        own = jnp.take(terms, asked.reshape(-1), axis=1, mode="clip").reshape(half, -1, cap).transpose(1, 0, 2)
+        got = jnp.concatenate([exchange(own), got2[:, :half]], axis=1)
+        return final(got, codes(count2, seed_list, cap, jax.ShapeDtypeStruct), bias2, fanout_one)
+
+    return lax.cond(flag[0, cap - 1] > 0.5, in_full, lambda logits: logits, logits)
 
 
 def solution(mesh):

time: 80.5 us -> 74.9 us (0.930)
  blocking collectives: 14.4 us -> 0 us
  starting transfers between devices: 6.2 us -> 13.5 us
  waiting for transfers between devices: 23.1 us -> 19.8 us
  Pallas kernels: 35.7 us -> 38.5 us
  local copies, waits for them, and re-layouts: 0.54 us -> 1.75 us
    all_to_all x1 -> x0, blocking collectives: 14.4 us -> none  [exchange(): return lax.all_to_all(blocks, AXES, split_axis=0, concat_axis=0, tiled=True)]
    pallas_call x2 -> x4, Pallas kernels: 9.56 us -> 17 us  [the longest x1 8.44 us: layer(): pl.pallas_call(functools.partial(layer_kernel, fanout), out_shape=(pltpu....]
    all_to_all x2 -> x3, starting transfers between devices: 6.2 us -> 13.5 us  [exchange(): return lax.all_to_all(blocks, AXES, split_axis=0, concat_axis=0, tiled=True)]
    pallas_call x3 -> x2, Pallas kernels: 18.8 us -> 14.1 us  [codes(): pl.pallas_call(functools.partial(codes_kernel, own_weight(depth - 1), cap...]
    all_to_all x2 -> x3, waiting for transfers between devices: 23.1 us -> 19.8 us  [exchange(): return lax.all_to_all(blocks, AXES, split_axis=0, concat_axis=0, tiled=True)]
  transfers between devices with their start and end apart: 2 -> 3, of which waited for: 2 -> 3; matrix products, arithmetic and copies ran while one was open for 1% -> 1% of each run, Pallas kernels for 23% -> 28%
where the time goes in v3:
time: 74.9 us; the launch traced here: 74.4 us
  Pallas kernels  38.5 us (51%)
  waiting for transfers between devices  19.8 us (26%)
  starting transfers between devices  13.5 us (18%)
  local copies, waits for them, and re-layouts  1.75 us (2%)
  between operations  0.87 us (1%)
    all_to_all x3, waiting for transfers between devices, exchange(): return lax.all_to_all(blocks, AXES, split_axis=0, concat_axis=0, tiled=True)  19.8 us
    pallas_call x2, Pallas kernels, codes(): pl.pallas_call(functools.partial(codes_kernel, own_weight(depth - 1), cap...  14.1 us
    all_to_all x3, starting transfers between devices, exchange(): return lax.all_to_all(blocks, AXES, split_axis=0, concat_axis=0, tiled=True)  13.5 us
    pallas_call x1, Pallas kernels, layer(): pl.pallas_call(functools.partial(layer_kernel, fanout), out_shape=(pltpu....  8.44 us
    pallas_call x1, Pallas kernels, fetch(): pl.pallas_call(functools.partial(fetch_kernel, parts, parts, group), out_...  7.45 us
    pallas_call x1, Pallas kernels, rank_codes(): pl.pallas_call(functools.partial(rank_codes_kernel, own_weight(depth - 1)...  5.83 us
  transfers between devices with their start and end apart: 3, of which 3 were waited for; matrix products, arithmetic and copies ran while one was open for 1% of the time, Pallas kernels for 28%

profile of v3, /device:TPU:0, one launch (start us, length us, event | category | flops | bytes accessed | tf_op | source)
XLA Modules:
  0.0 74.4 jit_solution(14090831187882556511)
XLA Ops:
  0.0 7.3 %all-to-all-start.2 = ((s32[32,1,128]{2,1,0:T(1,128)}), s32[32,1,128]{2,1,0:T(1,128)S(1)}, u32[]{:S(2)}, u32[]{:S(2)}) async-start(s32[32,1,128]{2,1,0:T(1,128)} %bitcast.15), calls=%async_computation.2 | async-start | bytes 32768 | tf_op jit(solution)/shard_map/all_to_all | solution.py:20
  7.3 1.2 %ask.1 = (f32[32,8,128]{2,1,0:T(8,128)S(1)}, f32[1,256]{1,0:T(1,128)S(1)}) custom-call(s32[32,128]{1,0:T(8,128)} %req2_ref.1, s32[16,256]{1,0:T(8,128)} %list_ref.1), custom_call_target="tpu_custom_call" | custom-call | tf_op jit(solution)/shard_map/ask/pallas_call | solution.py:180
  8.6 0.6 copy-done
  9.2 5.2 %all-to-all-done.2 = s32[32,1,128]{2,1,0:T(1,128)S(1)} async-done(((s32[32,1,128]{2,1,0:T(1,128)}), s32[32,1,128]{2,1,0:T(1,128)S(1)}, u32[]{:S(2)}, u32[]{:S(2)}) %all-to-all-start.2) | async-done | bytes 16416 | tf_op jit(solution)/shard_map/all_to_all | solution.py:20
  14.4 7.4 %fetch.1 = bf16[32,104,128]{2,1,0:T(8,128)(2,1)} custom-call(s32[32,128]{1,0:T(8,128)S(1)} %bitcast.12, f32[32,8,128]{2,1,0:T(8,128)} %copy-done, bf16[100,19456]{1,0:T(8,128)(2,1)} %table_hbm.1), custom_call_target="tpu_custom_call" | custom-call | tf_op jit(solution)/shard_map/fetch/pallas_call | solution.py:113
  21.9 2.6 %all-to-all-start.3 = ((bf16[32,104,128]{2,1,0:T(8,128)(2,1)}), bf16[32,104,128]{2,1,0:T(8,128)(2,1)S(1)}, u32[]{:S(2)}, u32[]{:S(2)}) async-start(bf16[32,104,128]{2,1,0:T(8,128)(2,1)} %fetch.1), calls=%async_computation.3 | async-start | bytes 1703936 | tf_op jit(solution)/shard_map/all_to_all | solution.py:20
  24.6 0.0 copy-done.1
  24.6 10.5 %codes.5.codes_hbm = bf16[3,4096,256]{2,1,0:T(8,128)(2,1)} custom-call(s32[32]{0:T(128)S(1)} %copy-done.1, s32[11,768]{1,0:T(8,128)S(1)} %slice.13.list_ref), custom_call_target="tpu_custom_call" | custom-call | tf_op jit(solution)/shard_map/codes/pallas_call | solution.py:225
  35.1 0.0 copy-start.8
  35.2 3.5 %codes.4.first_ref = bf16[1,4096,256]{2,1,0:T(8,128)(2,1)S(1)} custom-call(s32[32]{0:T(128)S(1)} %copy-done.1, s32[11,256]{1,0:T(8,128)S(1)} %slice.12.list_ref), custom_call_target="tpu_custom_call" | custom-call | tf_op jit(solution)/shard_map/codes/pallas_call | solution.py:225
  38.7 0.1 copy.34.b_ref
  38.8 0.1 copy.32.ws_ref
  39.0 0.1 copy.33.wn_ref
  39.1 0.0 copy-start.10
  39.2 0.0 copy-start.2
  39.2 0.0 copy-start.9
  39.2 7.4 %all-to-all-done.3.got_ref = bf16[32,104,128]{2,1,0:T(8,128)(2,1)S(1)} async-done(((bf16[32,104,128]{2,1,0:T(8,128)(2,1)}), bf16[32,104,128]{2,1,0:T(8,128)(2,1)S(1)}, u32[]{:S(2)}, u32[]{:S(2)}) %all-to-all-start.3) | async-done | bytes 852000 | tf_op jit(solution)/shard_map/all_to_all | solution.py:20
  46.5 8.4 %layer.1 = (bf16[32,56,128]{2,1,0:T(8,128)(2,1)}, bf16[48,1024]{1,0:T(8,128)(2,1)}, f32[1,128]{1,0:T(1,128)S(1)}) custom-call(bf16[32,104,128]{2,1,0:T(8,128)(2,1)S(1)} %all-to-all-done.3.got_ref, bf16[1,4096,256]{2,1,0:T(8,128)(2,1)S(1)} %codes.4.first_ref, bf16[3,4096,256]{2,1,0:T(8,128)(2,1)} %codes.5.codes_hbm, bf16[256,100]{1,0:T(8,128)(2,1)S(1)} %copy.32.ws_ref, ...), custom_call_target="tpu_custom_call" | custom-call | tf_op jit(solution)/shard_map/layer/pallas_call | solution.py:368
  55.0 3.5 %all-to-all-start.4 = ((bf16[32,56,128]{2,1,0:T(8,128)(2,1)}), bf16[32,56,128]{2,1,0:T(8,128)(2,1)S(1)}, u32[]{:S(2)}, u32[]{:S(2)}) async-start(bf16[32,56,128]{2,1,0:T(8,128)(2,1)} %get-tuple-element.34), calls=%async_computation.4 | async-start | bytes 917504 | tf_op jit(solution)/shard_map/all_to_all | solution.py:20
  58.5 0.1 copy.35.b_ref
  58.7 5.8 %rank_codes.1.code_ref = bf16[4096,256]{1,0:T(8,128)(2,1)S(1)} custom-call(s32[32]{0:T(128)S(1)} %copy-done.9, s32[16,256]{1,0:T(8,128)S(1)} %copy-done.2, f32[1,256]{1,0:T(1,128)S(1)} %get-tuple-element.35.rank_ref), custom_call_target="tpu_custom_call" | custom-call | tf_op jit(solution)/shard_map/rank_codes/pallas_call | solution.py:266
  64.5 0.6 slice.14
  65.7 7.2 %all-to-all-done.4.got_ref = bf16[32,56,128]{2,1,0:T(8,128)(2,1)S(1)} async-done(((bf16[32,56,128]{2,1,0:T(8,128)(2,1)}), bf16[32,56,128]{2,1,0:T(8,128)(2,1)S(1)}, u32[]{:S(2)}, u32[]{:S(2)}) %all-to-all-start.4) | async-done | bytes 458784 | tf_op jit(solution)/shard_map/all_to_all | solution.py:20
  73.0 1.5 %rank_logits.1 = f32[47,256]{1,0:T(8,128)} custom-call(bf16[32,56,128]{2,1,0:T(8,128)(2,1)S(1)} %all-to-all-done.4.got_ref, bf16[4096,256]{1,0:T(8,128)(2,1)S(1)} %rank_codes.1.code_ref, f32[47,1]{1,0:T(8,128)S(1)} %copy.35.b_ref), custom_call_target="tpu_custom_call" | custom-call | tf_op jit(solution)/shard_map/rank_logits/pallas_call | solution.py:503
  (22 shorter events, 0.1 us)
Async XLA Ops:
  0.0 14.4 %all-to-all-start.2 = ((s32[32,1,128]{2,1,0:T(1,128)}), s32[32,1,128]{2,1,0:T(1,128)S(1)}, u32[]{:S(2)}, u32[]{:S(2)}) async-start(s32[32,1,128]{2,1,0:T(1,128)} %bitcast.15), calls=%async_computation.2 | async-start | bytes 32768 | tf_op jit(solution)/shard_map/all_to_all | solution.py:20
  8.5 0.6 copy-start
  14.4 10.1 %copy-start.4 = (s32[11,1024]{1,0:T(8,128)S(1)}, s32[11,1024]{1,0:T(8,128)}, u32[]{:S(2)}) copy-start(s32[11,1024]{1,0:T(8,128)} %param.18) | copy-start | bytes 135172
  14.4 10.1 %copy-start.1 = (s32[32]{0:T(128)S(1)}, s32[32]{0:T(128)}, u32[]{:S(2)}) copy-start(s32[32]{0:T(128)} %count_ref.4) | copy-start | bytes 388
  21.9 24.6 %all-to-all-start.3 = ((bf16[32,104,128]{2,1,0:T(8,128)(2,1)}), bf16[32,104,128]{2,1,0:T(8,128)(2,1)S(1)}, u32[]{:S(2)}, u32[]{:S(2)}) async-start(bf16[32,104,128]{2,1,0:T(8,128)(2,1)} %fetch.1), calls=%async_computation.3 | async-start | bytes 1703936 | tf_op jit(solution)/shard_map/all_to_all | solution.py:20
  35.1 3.6 %copy-start.11 = (f32[256]{0:T(256)S(1)}, f32[256]{0:T(256)}, u32[]{:S(2)}) copy-start(f32[256]{0:T(256)} %param.24) | copy-start | bytes 3076
  35.1 3.7 %copy-start.5 = (bf16[256,100]{0,1:T(8,128)(2,1)S(1)}, bf16[256,100]{0,1:T(8,128)(2,1)}, u32[]{:S(2)}) copy-start(bf16[256,100]{0,1:T(8,128)(2,1)} %param.22) | copy-start | bytes 153604
  35.1 3.8 %copy-start.6 = (bf16[256,100]{0,1:T(8,128)(2,1)S(1)}, bf16[256,100]{0,1:T(8,128)(2,1)}, u32[]{:S(2)}) copy-start(bf16[256,100]{0,1:T(8,128)(2,1)} %param.23) | copy-start | bytes 153604
  35.1 4.0 %copy-start.7 = (bf16[47,256]{1,0:T(8,128)(2,1)S(1)}, bf16[47,256]{1,0:T(8,128)(2,1)}, u32[]{:S(2)}) copy-start(bf16[47,256]{1,0:T(8,128)(2,1)} %param.26) | copy-start | bytes 72196
  35.1 4.0 %copy-start.8 = (bf16[47,256]{1,0:T(8,128)(2,1)S(1)}, bf16[47,256]{1,0:T(8,128)(2,1)}, u32[]{:S(2)}) copy-start(bf16[47,256]{1,0:T(8,128)(2,1)} %param.25) | copy-start | bytes 72196
  39.1 19.4 %copy-start.10 = (f32[47]{0:T(128)S(1)}, f32[47]{0:T(128)}, u32[]{:S(2)}) copy-start(f32[47]{0:T(128)} %param.27) | copy-start | bytes 568
  39.2 19.5 %copy-start.2 = (s32[16,256]{1,0:T(8,128)S(1)}, s32[16,256]{1,0:T(8,128)}, u32[]{:S(2)}) copy-start(s32[16,256]{1,0:T(8,128)} %list_ref.1) | copy-start | bytes 49156
  39.2 19.5 %copy-start.9 = (s32[32]{0:T(128)S(1)}, s32[32]{0:T(128)}, u32[]{:S(2)}) copy-start(s32[32]{0:T(128)} %count_ref.5) | copy-start | bytes 388
  55.0 18.0 %all-to-all-start.4 = ((bf16[32,56,128]{2,1,0:T(8,128)(2,1)}), bf16[32,56,128]{2,1,0:T(8,128)(2,1)S(1)}, u32[]{:S(2)}, u32[]{:S(2)}) async-start(bf16[32,56,128]{2,1,0:T(8,128)(2,1)} %get-tuple-element.34), calls=%async_computation.4 | async-start | bytes 917504 | tf_op jit(solution)/shard_map/all_to_all | solution.py:20
  58.6 15.8 %copy-start.3 = (bf16[48,1024]{1,0:T(8,128)(2,1)S(1)}, bf16[48,1024]{1,0:T(8,128)(2,1)}, u32[]{:S(2)}) copy-start(bf16[48,1024]{1,0:T(8,128)(2,1)} %get-tuple-element.36) | copy-start | bytes 294916

commit v4 on v3

--- a/solution.py
+++ b/solution.py
@@ -30,49 +30,70 @@
     return jnp.where(rows == lanes, 1.0, 0.0).astype(dtype)
 
 
+def head_kernel(parts, table_hbm, out_ref, cols, sems):
+    feats, n = cols.shape
+    span = n // parts
+    loads = [
+        pltpu.make_async_copy(table_hbm.at[:, pl.ds(i * span, span)], cols.at[:, pl.ds(i * span, span)], sems.at[i])
+        for i in range(parts)
+    ]
+    for c in loads:
+        c.start()
+    for i in range(parts):
+        loads[i].wait()
+        for at in range(i * span, (i + 1) * span, 128):
+            out_ref[at : at + 128, :feats] = cols[:, at : at + 128].T.astype(F32)
+
+
+def head_rows(table_t, n):
+    feats = table_t.shape[0]
+    return pl.pallas_call(
+        functools.partial(head_kernel, 4),
+        out_shape=jax.ShapeDtypeStruct((n, 128), F32),
+        in_specs=[IN_HBM],
+        out_specs=WHOLE_VMEM,
+        scratch_shapes=[pltpu.VMEM((feats, n), BF16), pltpu.SemaphoreType.DMA((4,))],
+        compiler_params=params(16),
+        name="head_rows",
+    )(pltpu.with_memory_space_constraint(table_t, pltpu.HBM))
+
+
 def fetch_kernel(
-    parts, ahead, group, idx_ref, extra_hbm, table_hbm, out_hbm, cols, rows, even, odd, slots, out_v, extra_v, sems, out_sems, slot_sems
+    parts, group, idx_ref, head_ref, extra_hbm, table_hbm, out_hbm, cols, rows, bufs, idx_s, out_v, extra_v, sems, out_sems
 ):
     feats, n = cols.shape
+    head = head_ref.shape[0]
     blocks, rows_out, cap = out_v.shape
     span = n // parts
     loads = [
         pltpu.make_async_copy(
-            table_hbm.at[:, pl.ds(i * span, span)], cols.at[:, pl.ds(i * span, span)], sems.at[i]
+            table_hbm.at[:, pl.ds(head + i * span, span)], cols.at[:, pl.ds(i * span, span)], sems.at[i]
         )
         for i in range(parts)
     ]
-    for c in loads[:ahead]:
+    for c in loads:
         c.start()
 
-    def refill(slot, first):
-        return pltpu.make_async_copy(idx_ref.at[pl.ds(first, group)], slots[slot], slot_sems.at[slot])
-
-    refill(0, 0).start()
-    refill(1, group).start()
+    to_scalar = pltpu.make_async_copy(idx_ref, idx_s, sems.at[parts + 1])
+    to_scalar.start()
     ask = pltpu.make_async_copy(extra_hbm, extra_v, sems.at[parts])
     ask.start()
-    wide = max(w for w in range(1, 9) if (span // 128) % w == 0)
+    take = pltpu.make_async_copy(head_ref, rows.at[pl.ds(0, head)], sems.at[parts + 2])
+    take.start()
     for i in range(parts):
-        if i + ahead < parts:
-            loads[i + ahead].start()
         loads[i].wait()
-
-        def tile(t, _):
-            for u in range(wide):
-                at = pl.multiple_of(i * span + (t * wide + u) * 128, 128)
-                rows[pl.ds(at, 128), :feats] = cols[:, pl.ds(at, 128)].astype(F32).T
-            return 0
-
-        lax.fori_loop(0, span // 128 // wide, tile, 0, unroll=True)
-
+        for at in range(i * span, (i + 1) * span, 128):
+            rows[head + at : head + at + 128, :feats] = cols[:, at : at + 128].T.astype(F32)
+
+    take.wait()
+    to_scalar.wait()
     ask.wait()
     base = feats // 8 * 8
     row = lax.broadcasted_iota(I32, (8, cap), 0)
 
-    def gather(slot, u, buf):
+    def gather(r, buf):
         for j in range(cap):
-            buf[pl.ds(j, 1), :] = rows[pl.ds(slots[slot][u, j], 1), :]
+            buf[pl.ds(j, 1), :] = rows[pl.ds(idx_s[r, j], 1), :]
 
     def turn(r, buf):
         y = buf[...].T
@@ -82,54 +103,42 @@
     def leave(i):
         return pltpu.make_async_copy(out_v.at[pl.ds(i * group, group)], out_hbm.at[pl.ds(i * group, group)], out_sems.at[i])
 
-    trips = blocks // (2 * group)
-
-    def many(i, _):
-        for slot in range(2):
-            first = (2 * i + slot) * group
-            refill(slot, first).wait()
-            for u in range(group):
-                buf = (even, odd)[u % 2]
-                gather(slot, u, buf)
-                turn(first + u, buf)
-
-            @pl.when(i + 1 < trips)
-            def _():
-                refill(slot, first + 2 * group).start()
-
-            leave(2 * i + slot).start()
-        return 0
-
-    lax.fori_loop(0, trips, many, 0)
-    for i in range(2 * trips):
+    for r in range(blocks):
+        gather(r, bufs[r % len(bufs)])
+        if r:
+            turn(r - 1, bufs[(r - 1) % len(bufs)])
+        if r and r % group == 0:
+            leave(r // group - 1).start()
+    turn(blocks - 1, bufs[(blocks - 1) % len(bufs)])
+    leave(blocks // group - 1).start()
+    for i in range(blocks // group):
         leave(i).wait()
 
 
-def fetch(idx, extra, table_t):
+def fetch(idx, extra, table_t, head):
     feats, n = table_t.shape
+    left = n - head.shape[0]
     blocks, cap = idx.shape
-    parts = 8 if n % 1024 == 0 else 1
+    parts = max(p for p in range(1, 9) if left // 128 % p == 0)
     group = 4
     return pl.pallas_call(
-        functools.partial(fetch_kernel, parts, parts, group),
+        functools.partial(fetch_kernel, parts, group),
         out_shape=pltpu.HBM((blocks, feats + 4, cap), BF16),
-        in_specs=[WHOLE_VMEM, IN_HBM, IN_HBM],
+        in_specs=[WHOLE_VMEM, WHOLE_VMEM, IN_HBM, IN_HBM],
         out_specs=IN_HBM,
         scratch_shapes=[
-            pltpu.VMEM((feats, n), BF16),
+            pltpu.VMEM((feats, left), BF16),
             pltpu.VMEM((n, 128), F32),
-            pltpu.VMEM((cap, 128), F32),
-            pltpu.VMEM((cap, 128), F32),
-            [pltpu.SMEM((group, cap), I32), pltpu.SMEM((group, cap), I32)],
+            [pltpu.VMEM((cap, 128), F32) for _ in range(4)],
+            pltpu.SMEM((blocks, cap), I32),
             pltpu.VMEM((blocks, feats + 4, cap), BF16),
             pltpu.VMEM((blocks, 8, cap), F32),
-            pltpu.SemaphoreType.DMA((parts + 1,)),
+            pltpu.SemaphoreType.DMA((parts + 3,)),
             pltpu.SemaphoreType.DMA((blocks // group,)),
-            pltpu.SemaphoreType.DMA((2,)),
         ],
         compiler_params=params(40),
         name="fetch",
-    )(idx, pltpu.with_memory_space_constraint(extra, pltpu.HBM), pltpu.with_memory_space_constraint(table_t, pltpu.HBM))
+    )(idx, head, pltpu.with_memory_space_constraint(extra, pltpu.HBM), pltpu.with_memory_space_constraint(table_t, pltpu.HBM))
 
 
 PARTS = 6
@@ -180,7 +189,7 @@
     return pl.pallas_call(
         functools.partial(ask_kernel, feats % 8),
         out_shape=(
-            jax.ShapeDtypeStruct((blocks, 8, cap), F32),
+            pltpu.HBM((blocks, 8, cap), F32),
             jax.ShapeDtypeStruct((1, seed_list.shape[1]), F32),
         ),
         in_specs=[WHOLE_VMEM, WHOLE_VMEM],
@@ -286,7 +295,6 @@
     rest, slots, width = codes_v.shape
     parts = rest + 1
     pairs, nodes = blocks // 2, choose_v.shape[1]
-    chunks = -(-blocks // PARTS)
     half = w2_ref.shape[0] // 2
     deep = half // PARTS
     own_w = own_weight(fanout)
@@ -295,16 +303,16 @@
 
     for q in range(rest):
         load(q).start()
-    one, zero = jnp.ones((16, cap), BF16), jnp.zeros((16, cap), BF16)
-
-    def fill(asked, p, u):
+    one, zero = jnp.ones((16, 2 * cap), BF16), jnp.zeros((16, 2 * cap), BF16)
+
+    def fill(asked, p):
         for base in range(0, nodes, 256):
             local = asked - base
             local = jnp.where((local >= 0) & (local < 256), local, -1.0)
-            want = jnp.broadcast_to(local, (16, cap)).astype(BF16)
+            want = jnp.broadcast_to(local, (16, 2 * cap)).astype(BF16)
             for g in range(0, 256, 16):
-                node = (lax.broadcasted_iota(I32, (16, cap), 0) + g).astype(F32).astype(BF16)
-                choose_v[p, base + g : base + g + 16, u * cap : (u + 1) * cap] = jnp.where(want == node, one, zero)
+                node = (lax.broadcasted_iota(I32, (16, 2 * cap), 0) + g).astype(F32).astype(BF16)
+                choose_v[p, base + g : base + g + 16, :] = jnp.where(want == node, one, zero)
 
     def asked_of(o, row):
         asked = got_ref[o, feats : feats + 4].astype(F32)
@@ -314,23 +322,27 @@
         for u in range(2):
             o = 2 * p + u
             got_v[:, pl.ds(pl.multiple_of(o * cap, cap), cap)] = got_ref[o, :feats]
-            fill(asked_of(o, 0), p, u)
+        fill(jnp.concatenate([asked_of(2 * p, 0), asked_of(2 * p + 1, 0)], axis=1), p)
         return 0
 
     lax.fori_loop(0, pairs, choose, 0)
     part, _ = lane_part((1, cap), cap)
-    for c in range(chunks):
-        asked = jnp.full((1, cap), -1.0, F32)
-        for u in range(min(PARTS, blocks - c * PARTS)):
-            asked = jnp.where(part == u, asked_of(c * PARTS + u, 2), asked)
-        fill(asked, pairs + c // 2, c % 2)
+    for p in range(pairs, choose_v.shape[0]):
+        both = []
+        for c in (2 * (p - pairs), 2 * (p - pairs) + 1):
+            asked = jnp.full((1, cap), -1.0, F32)
+            for u in range(max(0, min(PARTS, blocks - c * PARTS))):
+                asked = jnp.where(part == u, asked_of(c * PARTS + u, 2), asked)
+            both.append(asked)
+        fill(jnp.concatenate(both, axis=1), p)
     flag = got_ref[0, feats + 2 : feats + 3].astype(F32)
     for o in range(1, blocks):
         flag = jnp.maximum(flag, got_ref[o, feats + 2 : feats + 3].astype(F32))
     flag_ref[...] = flag
     for q in range(parts):
-        if q:
-            load(q - 1).wait()
+        if q == 1:
+            for k in range(rest):
+                load(k).wait()
         code = codes_v[q - 1] if q else first_ref[0]
         both = jnp.dot(got_v[...], code, preferred_element_type=F32)
         own = jnp.dot(got_v[...], split_codes(code, own_w), preferred_element_type=F32)
@@ -510,6 +522,7 @@
     )(got, code, bias2[:, None])
 
 
+HEAD = 6144
 MOST = 8 << 20
 
 
@@ -530,6 +543,7 @@
 ):
     cap = req_rows.shape[1]
     fits = req_rows.size * frontier_list.shape[1] <= MOST and req2_rows.shape[1] == cap and table_t.shape[0] % 8 == 4
+    fits = fits and table_t.shape[1] % 128 == 0 and table_t.shape[1] > HEAD
     if not fits or table_t.shape[1] > 32768 or frontier_list.shape[1] > 65536:
         return plain_body(
             table_t,
@@ -548,7 +562,7 @@
         )
     feats, fanout_two, fanout_one = table_t.shape[0], frontier_list.shape[0] - 1, seed_list.shape[0] - 1
     extra, rank = ask(req2_rows, seed_list, feats)
-    got1 = exchange(fetch(exchange(req_rows), extra, table_t))
+    got1 = exchange(fetch(exchange(req_rows), extra, table_t, head_rows(table_t, HEAD)))
     first = codes(count1, frontier_list[:, :256], cap, jax.ShapeDtypeStruct)
     code1 = codes(count1, frontier_list[:, 256:], cap, pltpu.HBM)
     classes = w2_self.shape[0]

time: 74.9 us -> 73.2 us (0.977)
  waiting for transfers between devices: 19.8 us -> 18.1 us
    all_to_all x3, waiting for transfers between devices: 19.8 us -> 18.1 us  [exchange(): return lax.all_to_all(blocks, AXES, split_axis=0, concat_axis=0, tiled=True)]
    pallas_call x2 -> x3, Pallas kernels: 8.66 us -> 9.76 us  [the longest x1 6.25 us: fetch(): pl.pallas_call(functools.partial(fetch_kernel, parts, group), out_shape=p...]
  transfers between devices with their start and end apart: 3 -> 3, of which waited for: 3 -> 3; matrix products, arithmetic and copies ran while one was open for 1% -> 1% of each run, Pallas kernels for 28% -> 32%
where the time goes in v4:
time: 73.2 us; the launch traced here: 72.8 us
  Pallas kernels  39.2 us (54%)
  waiting for transfers between devices  18.1 us (25%)
  starting transfers between devices  13.5 us (18%)
  local copies, waits for them, and re-layouts  1.12 us (2%)
  between operations  0.87 us (1%)
    all_to_all x3, waiting for transfers between devices, exchange(): return lax.all_to_all(blocks, AXES, split_axis=0, concat_axis=0, tiled=True)  18.1 us
    pallas_call x2, Pallas kernels, codes(): pl.pallas_call(functools.partial(codes_kernel, own_weight(depth - 1), cap...  14.1 us
    all_to_all x3, starting transfers between devices, exchange(): return lax.all_to_all(blocks, AXES, split_axis=0, concat_axis=0, tiled=True)  13.5 us
    pallas_call x1, Pallas kernels, layer(): pl.pallas_call(functools.partial(layer_kernel, fanout), out_shape=(pltpu....  8.02 us
    pallas_call x1, Pallas kernels, fetch(): pl.pallas_call(functools.partial(fetch_kernel, parts, group), out_shape=p...  6.25 us
    pallas_call x1, Pallas kernels, rank_codes(): pl.pallas_call(functools.partial(rank_codes_kernel, own_weight(depth - 1)...  5.83 us
    pallas_call x1, Pallas kernels, ask(): pl.pallas_call(functools.partial(ask_kernel, feats % 8), out_shape=(pltpu...  1.83 us
    pallas_call x1, Pallas kernels, head_rows(): pl.pallas_call(functools.partial(head_kernel, 4), out_shape=jax.ShapeDtyp...  1.68 us
  transfers between devices with their start and end apart: 3, of which 3 were waited for; matrix products, arithmetic and copies ran while one was open for 1% of the time, Pallas kernels for 32%

profile of v4, /device:TPU:0, one launch (start us, length us, event | category | flops | bytes accessed | tf_op | source)
XLA Modules:
  0.0 72.8 jit_solution(3564262946192130431)
XLA Ops:
  0.0 7.3 %all-to-all-start.2 = ((s32[32,1,128]{2,1,0:T(1,128)}), s32[32,1,128]{2,1,0:T(1,128)S(1)}, u32[]{:S(2)}, u32[]{:S(2)}) async-start(s32[32,1,128]{2,1,0:T(1,128)} %bitcast.15), calls=%async_computation.2 | async-start | bytes 32768 | tf_op jit(solution)/shard_map/all_to_all | solution.py:20
  7.3 0.0 copy-start.1
  7.3 1.7 %head_rows.1.head_ref = f32[6144,128]{1,0:T(8,128)S(1)} custom-call(bf16[100,19456]{1,0:T(8,128)(2,1)} %table_hbm.3), custom_call_target="tpu_custom_call" | custom-call | tf_op jit(solution)/shard_map/head_rows/pallas_call | solution.py:50
  9.0 1.8 %ask.1 = (f32[32,8,128]{2,1,0:T(8,128)}, f32[1,256]{1,0:T(1,128)S(1)}) custom-call(s32[32,128]{1,0:T(8,128)} %req2_ref.1, s32[16,256]{1,0:T(8,128)S(1)} %copy-done.1), custom_call_target="tpu_custom_call" | custom-call | tf_op jit(solution)/shard_map/ask/pallas_call | solution.py:189
  10.9 3.6 %all-to-all-done.2 = s32[32,1,128]{2,1,0:T(1,128)S(1)} async-done(((s32[32,1,128]{2,1,0:T(1,128)}), s32[32,1,128]{2,1,0:T(1,128)S(1)}, u32[]{:S(2)}, u32[]{:S(2)}) %all-to-all-start.2) | async-done | bytes 16416 | tf_op jit(solution)/shard_map/all_to_all | solution.py:20
  14.4 6.2 %fetch.1 = bf16[32,104,128]{2,1,0:T(8,128)(2,1)} custom-call(s32[32,128]{1,0:T(8,128)S(1)} %bitcast.12, f32[6144,128]{1,0:T(8,128)S(1)} %head_rows.1.head_ref, f32[32,8,128]{2,1,0:T(8,128)} %get-tuple-element.32.extra_hbm, bf16[100,19456]{1,0:T(8,128)(2,1)} %table_hbm.3), custom_call_target="tpu_custom_call" | custom-call | tf_op jit(solution)/shard_map/fetch/pallas_call | solution.py:124
  20.7 2.6 %all-to-all-start.3 = ((bf16[32,104,128]{2,1,0:T(8,128)(2,1)}), bf16[32,104,128]{2,1,0:T(8,128)(2,1)S(1)}, u32[]{:S(2)}, u32[]{:S(2)}) async-start(bf16[32,104,128]{2,1,0:T(8,128)(2,1)} %fetch.1), calls=%async_computation.3 | async-start | bytes 1703936 | tf_op jit(solution)/shard_map/all_to_all | solution.py:20
  23.4 0.0 copy-done
  23.4 10.6 %codes.5.codes_hbm = bf16[3,4096,256]{2,1,0:T(8,128)(2,1)} custom-call(s32[32]{0:T(128)S(1)} %copy-done, s32[11,768]{1,0:T(8,128)S(1)} %slice.13.list_ref), custom_call_target="tpu_custom_call" | custom-call | tf_op jit(solution)/shard_map/codes/pallas_call | solution.py:234
  34.0 0.0 copy-start.7
  34.0 3.5 %codes.4.first_ref = bf16[1,4096,256]{2,1,0:T(8,128)(2,1)S(1)} custom-call(s32[32]{0:T(128)S(1)} %copy-done, s32[11,256]{1,0:T(8,128)S(1)} %slice.12.list_ref), custom_call_target="tpu_custom_call" | custom-call | tf_op jit(solution)/shard_map/codes/pallas_call | solution.py:234
  37.5 0.1 copy.34.b_ref
  37.7 0.1 copy.32.ws_ref
  37.8 0.1 copy.33.wn_ref
  38.0 0.0 copy-start.9
  38.0 0.0 copy-start.8
  38.0 7.3 %all-to-all-done.3.got_ref = bf16[32,104,128]{2,1,0:T(8,128)(2,1)S(1)} async-done(((bf16[32,104,128]{2,1,0:T(8,128)(2,1)}), bf16[32,104,128]{2,1,0:T(8,128)(2,1)S(1)}, u32[]{:S(2)}, u32[]{:S(2)}) %all-to-all-start.3) | async-done | bytes 852000 | tf_op jit(solution)/shard_map/all_to_all | solution.py:20
  45.3 8.0 %layer.1 = (bf16[32,56,128]{2,1,0:T(8,128)(2,1)}, bf16[48,1024]{1,0:T(8,128)(2,1)}, f32[1,128]{1,0:T(1,128)S(1)}) custom-call(bf16[32,104,128]{2,1,0:T(8,128)(2,1)S(1)} %all-to-all-done.3.got_ref, bf16[1,4096,256]{2,1,0:T(8,128)(2,1)S(1)} %codes.4.first_ref, bf16[3,4096,256]{2,1,0:T(8,128)(2,1)} %codes.5.codes_hbm, bf16[256,100]{1,0:T(8,128)(2,1)S(1)} %copy.32.ws_ref, ...), custom_call_target="tpu_custom_call" | custom-call | tf_op jit(solution)/shard_map/layer/pallas_call | solution.py:380
  53.4 3.5 %all-to-all-start.4 = ((bf16[32,56,128]{2,1,0:T(8,128)(2,1)}), bf16[32,56,128]{2,1,0:T(8,128)(2,1)S(1)}, u32[]{:S(2)}, u32[]{:S(2)}) async-start(bf16[32,56,128]{2,1,0:T(8,128)(2,1)} %get-tuple-element.34), calls=%async_computation.4 | async-start | bytes 917504 | tf_op jit(solution)/shard_map/all_to_all | solution.py:20
  56.9 0.1 copy.35.b_ref
  57.0 5.8 %rank_codes.1.code_ref = bf16[4096,256]{1,0:T(8,128)(2,1)S(1)} custom-call(s32[32]{0:T(128)S(1)} %copy-done.8, s32[16,256]{1,0:T(8,128)S(1)} %copy-done.1, f32[1,256]{1,0:T(1,128)S(1)} %get-tuple-element.35.rank_ref), custom_call_target="tpu_custom_call" | custom-call | tf_op jit(solution)/shard_map/rank_codes/pallas_call | solution.py:275
  62.9 0.6 slice.14
  64.1 7.2 %all-to-all-done.4.got_ref = bf16[32,56,128]{2,1,0:T(8,128)(2,1)S(1)} async-done(((bf16[32,56,128]{2,1,0:T(8,128)(2,1)}), bf16[32,56,128]{2,1,0:T(8,128)(2,1)S(1)}, u32[]{:S(2)}, u32[]{:S(2)}) %all-to-all-start.4) | async-done | bytes 458784 | tf_op jit(solution)/shard_map/all_to_all | solution.py:20
  71.3 1.5 %rank_logits.1 = f32[47,256]{1,0:T(8,128)} custom-call(bf16[32,56,128]{2,1,0:T(8,128)(2,1)S(1)} %all-to-all-done.4.got_ref, bf16[4096,256]{1,0:T(8,128)(2,1)S(1)} %rank_codes.1.code_ref, f32[47,1]{1,0:T(8,128)S(1)} %copy.35.b_ref), custom_call_target="tpu_custom_call" | custom-call | tf_op jit(solution)/shard_map/rank_logits/pallas_call | solution.py:515
  (21 shorter events, 0.0 us)
Async XLA Ops:
  0.0 14.4 %all-to-all-start.2 = ((s32[32,1,128]{2,1,0:T(1,128)}), s32[32,1,128]{2,1,0:T(1,128)S(1)}, u32[]{:S(2)}, u32[]{:S(2)}) async-start(s32[32,1,128]{2,1,0:T(1,128)} %bitcast.15), calls=%async_computation.2 | async-start | bytes 32768 | tf_op jit(solution)/shard_map/all_to_all | solution.py:20
  7.3 1.7 %copy-start.1 = (s32[16,256]{1,0:T(8,128)S(1)}, s32[16,256]{1,0:T(8,128)}, u32[]{:S(2)}) copy-start(s32[16,256]{1,0:T(8,128)} %list_ref.1) | copy-start | bytes 49156
  14.4 8.9 %copy-start.3 = (s32[11,1024]{1,0:T(8,128)S(1)}, s32[11,1024]{1,0:T(8,128)}, u32[]{:S(2)}) copy-start(s32[11,1024]{1,0:T(8,128)} %param.18) | copy-start | bytes 135172
  14.4 8.9 %copy-start = (s32[32]{0:T(128)S(1)}, s32[32]{0:T(128)}, u32[]{:S(2)}) copy-start(s32[32]{0:T(128)} %count_ref.4) | copy-start | bytes 388
  20.7 24.6 %all-to-all-start.3 = ((bf16[32,104,128]{2,1,0:T(8,128)(2,1)}), bf16[32,104,128]{2,1,0:T(8,128)(2,1)S(1)}, u32[]{:S(2)}, u32[]{:S(2)}) async-start(bf16[32,104,128]{2,1,0:T(8,128)(2,1)} %fetch.1), calls=%async_computation.3 | async-start | bytes 1703936 | tf_op jit(solution)/shard_map/all_to_all | solution.py:20
  34.0 3.6 %copy-start.10 = (f32[256]{0:T(256)S(1)}, f32[256]{0:T(256)}, u32[]{:S(2)}) copy-start(f32[256]{0:T(256)} %param.24) | copy-start | bytes 3076
  34.0 3.7 %copy-start.4 = (bf16[256,100]{0,1:T(8,128)(2,1)S(1)}, bf16[256,100]{0,1:T(8,128)(2,1)}, u32[]{:S(2)}) copy-start(bf16[256,100]{0,1:T(8,128)(2,1)} %param.22) | copy-start | bytes 153604
  34.0 3.8 %copy-start.5 = (bf16[256,100]{0,1:T(8,128)(2,1)S(1)}, bf16[256,100]{0,1:T(8,128)(2,1)}, u32[]{:S(2)}) copy-start(bf16[256,100]{0,1:T(8,128)(2,1)} %param.23) | copy-start | bytes 153604
  34.0 4.0 %copy-start.6 = (bf16[47,256]{1,0:T(8,128)(2,1)S(1)}, bf16[47,256]{1,0:T(8,128)(2,1)}, u32[]{:S(2)}) copy-start(bf16[47,256]{1,0:T(8,128)(2,1)} %param.26) | copy-start | bytes 72196
  34.0 4.0 %copy-start.7 = (bf16[47,256]{1,0:T(8,128)(2,1)S(1)}, bf16[47,256]{1,0:T(8,128)(2,1)}, u32[]{:S(2)}) copy-start(bf16[47,256]{1,0:T(8,128)(2,1)} %param.25) | copy-start | bytes 72196
  38.0 18.9 %copy-start.9 = (f32[47]{0:T(128)S(1)}, f32[47]{0:T(128)}, u32[]{:S(2)}) copy-start(f32[47]{0:T(128)} %param.27) | copy-start | bytes 568
  38.0 19.0 %copy-start.8 = (s32[32]{0:T(128)S(1)}, s32[32]{0:T(128)}, u32[]{:S(2)}) copy-start(s32[32]{0:T(128)} %count_ref.5) | copy-start | bytes 388
  53.4 18.0 %all-to-all-start.4 = ((bf16[32,56,128]{2,1,0:T(8,128)(2,1)}), bf16[32,56,128]{2,1,0:T(8,128)(2,1)S(1)}, u32[]{:S(2)}, u32[]{:S(2)}) async-start(bf16[32,56,128]{2,1,0:T(8,128)(2,1)} %get-tuple-element.34), calls=%async_computation.4 | async-start | bytes 917504 | tf_op jit(solution)/shard_map/all_to_all | solution.py:20
  57.0 15.8 %copy-start.2 = (bf16[48,1024]{1,0:T(8,128)(2,1)S(1)}, bf16[48,1024]{1,0:T(8,128)(2,1)}, u32[]{:S(2)}) copy-start(bf16[48,1024]{1,0:T(8,128)(2,1)} %get-tuple-element.36) | copy-start | bytes 294916

commit v5 on v4

--- a/solution.py
+++ b/solution.py
@@ -103,14 +103,14 @@
     def leave(i):
         return pltpu.make_async_copy(out_v.at[pl.ds(i * group, group)], out_hbm.at[pl.ds(i * group, group)], out_sems.at[i])
 
-    for r in range(blocks):
-        gather(r, bufs[r % len(bufs)])
-        if r:
-            turn(r - 1, bufs[(r - 1) % len(bufs)])
-        if r and r % group == 0:
-            leave(r // group - 1).start()
-    turn(blocks - 1, bufs[(blocks - 1) % len(bufs)])
-    leave(blocks // group - 1).start()
+    for r in range(blocks + 1):
+        if r < blocks:
+            gather(r, bufs[r % len(bufs)])
+        done = r - 1
+        if done >= 0:
+            turn(done, bufs[done % len(bufs)])
+            if done % group == group - 1:
+                leave(done // group).start()
     for i in range(blocks // group):
         leave(i).wait()
 
@@ -129,7 +129,7 @@
         scratch_shapes=[
             pltpu.VMEM((feats, left), BF16),
             pltpu.VMEM((n, 128), F32),
-            [pltpu.VMEM((cap, 128), F32) for _ in range(4)],
+            [pltpu.VMEM((cap, 128), F32) for _ in range(8)],
             pltpu.SMEM((blocks, cap), I32),
             pltpu.VMEM((blocks, feats + 4, cap), BF16),
             pltpu.VMEM((blocks, 8, cap), F32),
@@ -522,7 +522,7 @@
     )(got, code, bias2[:, None])
 
 
-HEAD = 6144
+HEAD = 6656
 MOST = 8 << 20
 
 

time: 73.2 us -> 73 us (level)
  no operation moved by 1% of the time
where the time goes in v5:
time: 73 us; the launch traced here: 72.6 us
  Pallas kernels  39 us (53%)
  waiting for transfers between devices  18.1 us (25%)
  starting transfers between devices  13.5 us (18%)
  local copies, waits for them, and re-layouts  1.12 us (2%)
  between operations  0.87 us (1%)
    all_to_all x3, waiting for transfers between devices, exchange(): return lax.all_to_all(blocks, AXES, split_axis=0, concat_axis=0, tiled=True)  18.1 us
    pallas_call x2, Pallas kernels, codes(): pl.pallas_call(functools.partial(codes_kernel, own_weight(depth - 1), cap...  14.1 us
    all_to_all x3, starting transfers between devices, exchange(): return lax.all_to_all(blocks, AXES, split_axis=0, concat_axis=0, tiled=True)  13.5 us
    pallas_call x1, Pallas kernels, layer(): pl.pallas_call(functools.partial(layer_kernel, fanout), out_shape=(pltpu....  8.02 us
    pallas_call x1, Pallas kernels, fetch(): pl.pallas_call(functools.partial(fetch_kernel, parts, group), out_shape=p...  6 us
    pallas_call x1, Pallas kernels, rank_codes(): pl.pallas_call(functools.partial(rank_codes_kernel, own_weight(depth - 1)...  5.83 us
    pallas_call x1, Pallas kernels, ask(): pl.pallas_call(functools.partial(ask_kernel, feats % 8), out_shape=(pltpu...  1.83 us
    pallas_call x1, Pallas kernels, head_rows(): pl.pallas_call(functools.partial(head_kernel, 4), out_shape=jax.ShapeDtyp...  1.75 us
  transfers between devices with their start and end apart: 3, of which 3 were waited for; matrix products, arithmetic and copies ran while one was open for 1% of the time, Pallas kernels for 32%

profile of v5, /device:TPU:0, one launch (start us, length us, event | category | flops | bytes accessed | tf_op | source)
XLA Modules:
  0.0 72.6 jit_solution(11553746528144334817)
XLA Ops:
  0.0 7.3 %all-to-all-start.2 = ((s32[32,1,128]{2,1,0:T(1,128)}), s32[32,1,128]{2,1,0:T(1,128)S(1)}, u32[]{:S(2)}, u32[]{:S(2)}) async-start(s32[32,1,128]{2,1,0:T(1,128)} %bitcast.15), calls=%async_computation.2 | async-start | bytes 32768 | tf_op jit(solution)/shard_map/all_to_all | solution.py:20
  7.3 0.0 copy-start.1
  7.3 1.8 %head_rows.1.head_ref = f32[6656,128]{1,0:T(8,128)S(1)} custom-call(bf16[100,19456]{1,0:T(8,128)(2,1)} %table_hbm.3), custom_call_target="tpu_custom_call" | custom-call | tf_op jit(solution)/shard_map/head_rows/pallas_call | solution.py:50
  9.1 1.8 %ask.1 = (f32[32,8,128]{2,1,0:T(8,128)}, f32[1,256]{1,0:T(1,128)S(1)}) custom-call(s32[32,128]{1,0:T(8,128)} %req2_ref.1, s32[16,256]{1,0:T(8,128)S(1)} %copy-done.1), custom_call_target="tpu_custom_call" | custom-call | tf_op jit(solution)/shard_map/ask/pallas_call | solution.py:189
  10.9 3.5 %all-to-all-done.2 = s32[32,1,128]{2,1,0:T(1,128)S(1)} async-done(((s32[32,1,128]{2,1,0:T(1,128)}), s32[32,1,128]{2,1,0:T(1,128)S(1)}, u32[]{:S(2)}, u32[]{:S(2)}) %all-to-all-start.2) | async-done | bytes 16416 | tf_op jit(solution)/shard_map/all_to_all | solution.py:20
  14.4 6.0 %fetch.1 = bf16[32,104,128]{2,1,0:T(8,128)(2,1)} custom-call(s32[32,128]{1,0:T(8,128)S(1)} %bitcast.12, f32[6656,128]{1,0:T(8,128)S(1)} %head_rows.1.head_ref, f32[32,8,128]{2,1,0:T(8,128)} %get-tuple-element.32.extra_hbm, bf16[100,19456]{1,0:T(8,128)(2,1)} %table_hbm.3), custom_call_target="tpu_custom_call" | custom-call | tf_op jit(solution)/shard_map/fetch/pallas_call | solution.py:124
  20.5 2.6 %all-to-all-start.3 = ((bf16[32,104,128]{2,1,0:T(8,128)(2,1)}), bf16[32,104,128]{2,1,0:T(8,128)(2,1)S(1)}, u32[]{:S(2)}, u32[]{:S(2)}) async-start(bf16[32,104,128]{2,1,0:T(8,128)(2,1)} %fetch.1), calls=%async_computation.3 | async-start | bytes 1703936 | tf_op jit(solution)/shard_map/all_to_all | solution.py:20
  23.2 10.6 %codes.5.codes_hbm = bf16[3,4096,256]{2,1,0:T(8,128)(2,1)} custom-call(s32[32]{0:T(128)S(1)} %copy-done, s32[11,768]{1,0:T(8,128)S(1)} %slice.13.list_ref), custom_call_target="tpu_custom_call" | custom-call | tf_op jit(solution)/shard_map/codes/pallas_call | solution.py:234
  33.7 0.0 copy-start.7
  33.7 3.5 %codes.4.first_ref = bf16[1,4096,256]{2,1,0:T(8,128)(2,1)S(1)} custom-call(s32[32]{0:T(128)S(1)} %copy-done, s32[11,256]{1,0:T(8,128)S(1)} %slice.12.list_ref), custom_call_target="tpu_custom_call" | custom-call | tf_op jit(solution)/shard_map/codes/pallas_call | solution.py:234
  37.3 0.1 copy.34.b_ref
  37.4 0.1 copy.32.ws_ref
  37.6 0.1 copy.33.wn_ref
  37.7 0.0 copy-start.9
  37.7 0.0 copy-start.8
  37.7 7.3 %all-to-all-done.3.got_ref = bf16[32,104,128]{2,1,0:T(8,128)(2,1)S(1)} async-done(((bf16[32,104,128]{2,1,0:T(8,128)(2,1)}), bf16[32,104,128]{2,1,0:T(8,128)(2,1)S(1)}, u32[]{:S(2)}, u32[]{:S(2)}) %all-to-all-start.3) | async-done | bytes 852000 | tf_op jit(solution)/shard_map/all_to_all | solution.py:20
  45.1 8.0 %layer.1 = (bf16[32,56,128]{2,1,0:T(8,128)(2,1)}, bf16[48,1024]{1,0:T(8,128)(2,1)}, f32[1,128]{1,0:T(1,128)S(1)}) custom-call(bf16[32,104,128]{2,1,0:T(8,128)(2,1)S(1)} %all-to-all-done.3.got_ref, bf16[1,4096,256]{2,1,0:T(8,128)(2,1)S(1)} %codes.4.first_ref, bf16[3,4096,256]{2,1,0:T(8,128)(2,1)} %codes.5.codes_hbm, bf16[256,100]{1,0:T(8,128)(2,1)S(1)} %copy.32.ws_ref, ...), custom_call_target="tpu_custom_call" | custom-call | tf_op jit(solution)/shard_map/layer/pallas_call | solution.py:380
  53.1 3.5 %all-to-all-start.4 = ((bf16[32,56,128]{2,1,0:T(8,128)(2,1)}), bf16[32,56,128]{2,1,0:T(8,128)(2,1)S(1)}, u32[]{:S(2)}, u32[]{:S(2)}) async-start(bf16[32,56,128]{2,1,0:T(8,128)(2,1)} %get-tuple-element.34), calls=%async_computation.4 | async-start | bytes 917504 | tf_op jit(solution)/shard_map/all_to_all | solution.py:20
  56.7 0.1 copy.35.b_ref
  56.8 0.0 copy-done.8
  56.8 5.8 %rank_codes.1.code_ref = bf16[4096,256]{1,0:T(8,128)(2,1)S(1)} custom-call(s32[32]{0:T(128)S(1)} %copy-done.8, s32[16,256]{1,0:T(8,128)S(1)} %copy-done.1, f32[1,256]{1,0:T(1,128)S(1)} %get-tuple-element.35.rank_ref), custom_call_target="tpu_custom_call" | custom-call | tf_op jit(solution)/shard_map/rank_codes/pallas_call | solution.py:275
  62.6 0.6 slice.14
  63.9 7.2 %all-to-all-done.4.got_ref = bf16[32,56,128]{2,1,0:T(8,128)(2,1)S(1)} async-done(((bf16[32,56,128]{2,1,0:T(8,128)(2,1)}), bf16[32,56,128]{2,1,0:T(8,128)(2,1)S(1)}, u32[]{:S(2)}, u32[]{:S(2)}) %all-to-all-start.4) | async-done | bytes 458784 | tf_op jit(solution)/shard_map/all_to_all | solution.py:20
  71.1 1.5 %rank_logits.1 = f32[47,256]{1,0:T(8,128)} custom-call(bf16[32,56,128]{2,1,0:T(8,128)(2,1)S(1)} %all-to-all-done.4.got_ref, bf16[4096,256]{1,0:T(8,128)(2,1)S(1)} %rank_codes.1.code_ref, f32[47,1]{1,0:T(8,128)S(1)} %copy.35.b_ref), custom_call_target="tpu_custom_call" | custom-call | tf_op jit(solution)/shard_map/rank_logits/pallas_call | solution.py:515
  (21 shorter events, 0.0 us)
Async XLA Ops:
  0.0 14.4 %all-to-all-start.2 = ((s32[32,1,128]{2,1,0:T(1,128)}), s32[32,1,128]{2,1,0:T(1,128)S(1)}, u32[]{:S(2)}, u32[]{:S(2)}) async-start(s32[32,1,128]{2,1,0:T(1,128)} %bitcast.15), calls=%async_computation.2 | async-start | bytes 32768 | tf_op jit(solution)/shard_map/all_to_all | solution.py:20
  7.3 1.8 %copy-start.1 = (s32[16,256]{1,0:T(8,128)S(1)}, s32[16,256]{1,0:T(8,128)}, u32[]{:S(2)}) copy-start(s32[16,256]{1,0:T(8,128)} %list_ref.1) | copy-start | bytes 49156
  14.4 8.7 %copy-start.3 = (s32[11,1024]{1,0:T(8,128)S(1)}, s32[11,1024]{1,0:T(8,128)}, u32[]{:S(2)}) copy-start(s32[11,1024]{1,0:T(8,128)} %param.18) | copy-start | bytes 135172
  14.4 8.7 %copy-start = (s32[32]{0:T(128)S(1)}, s32[32]{0:T(128)}, u32[]{:S(2)}) copy-start(s32[32]{0:T(128)} %count_ref.4) | copy-start | bytes 388
  20.5 24.6 %all-to-all-start.3 = ((bf16[32,104,128]{2,1,0:T(8,128)(2,1)}), bf16[32,104,128]{2,1,0:T(8,128)(2,1)S(1)}, u32[]{:S(2)}, u32[]{:S(2)}) async-start(bf16[32,104,128]{2,1,0:T(8,128)(2,1)} %fetch.1), calls=%async_computation.3 | async-start | bytes 1703936 | tf_op jit(solution)/shard_map/all_to_all | solution.py:20
  33.7 3.6 %copy-start.10 = (f32[256]{0:T(256)S(1)}, f32[256]{0:T(256)}, u32[]{:S(2)}) copy-start(f32[256]{0:T(256)} %param.24) | copy-start | bytes 3076
  33.7 3.7 %copy-start.4 = (bf16[256,100]{0,1:T(8,128)(2,1)S(1)}, bf16[256,100]{0,1:T(8,128)(2,1)}, u32[]{:S(2)}) copy-start(bf16[256,100]{0,1:T(8,128)(2,1)} %param.22) | copy-start | bytes 153604
  33.7 3.8 %copy-start.5 = (bf16[256,100]{0,1:T(8,128)(2,1)S(1)}, bf16[256,100]{0,1:T(8,128)(2,1)}, u32[]{:S(2)}) copy-start(bf16[256,100]{0,1:T(8,128)(2,1)} %param.23) | copy-start | bytes 153604
  33.7 4.0 %copy-start.6 = (bf16[47,256]{1,0:T(8,128)(2,1)S(1)}, bf16[47,256]{1,0:T(8,128)(2,1)}, u32[]{:S(2)}) copy-start(bf16[47,256]{1,0:T(8,128)(2,1)} %param.26) | copy-start | bytes 72196
  33.7 4.0 %copy-start.7 = (bf16[47,256]{1,0:T(8,128)(2,1)S(1)}, bf16[47,256]{1,0:T(8,128)(2,1)}, u32[]{:S(2)}) copy-start(bf16[47,256]{1,0:T(8,128)(2,1)} %param.25) | copy-start | bytes 72196
  37.7 18.9 %copy-start.9 = (f32[47]{0:T(128)S(1)}, f32[47]{0:T(128)}, u32[]{:S(2)}) copy-start(f32[47]{0:T(128)} %param.27) | copy-start | bytes 568
  37.7 19.0 %copy-start.8 = (s32[32]{0:T(128)S(1)}, s32[32]{0:T(128)}, u32[]{:S(2)}) copy-start(s32[32]{0:T(128)} %count_ref.5) | copy-start | bytes 388
  53.1 18.0 %all-to-all-start.4 = ((bf16[32,56,128]{2,1,0:T(8,128)(2,1)}), bf16[32,56,128]{2,1,0:T(8,128)(2,1)S(1)}, u32[]{:S(2)}, u32[]{:S(2)}) async-start(bf16[32,56,128]{2,1,0:T(8,128)(2,1)} %get-tuple-element.34), calls=%async_computation.4 | async-start | bytes 917504 | tf_op jit(solution)/shard_map/all_to_all | solution.py:20
  56.8 15.8 %copy-start.2 = (bf16[48,1024]{1,0:T(8,128)(2,1)S(1)}, bf16[48,1024]{1,0:T(8,128)(2,1)}, u32[]{:S(2)}) copy-start(bf16[48,1024]{1,0:T(8,128)(2,1)} %get-tuple-element.36) | copy-start | bytes 294916
